TPU v7x, 32 devices: a 4x4x1 block of a 4x4x8 slice. The times are simulated.
32 devices in a mesh: dp: 1 (over z), tp: 4 (over y), cp: 8 (over x, core).
Axes of the slice: x: 4, y: 4, z: 1, core: 2. Of those that a mesh axis runs over, the one named last changes fastest.
The devices are a block of a 4x4x8 slice.
Arguments:
- hidden: bfloat16 [8192, 1024], P(('dp', 'cp'))
- positions: int32 [8192], P(('dp', 'cp'))
- ln_gain: bfloat16 [1024], replicated
- w_q: bfloat16 [1024, 2048], P(None, 'tp')
- w_k: bfloat16 [1024, 1024], P(None, 'tp')
- w_v: bfloat16 [1024, 1024], P(None, 'tp')
- w_o: bfloat16 [2048, 1024], P('tp')
- w_gate: bfloat16 [1024, 3072], P(None, 'tp')
- w_up: bfloat16 [1024, 3072], P(None, 'tp')
- w_down: bfloat16 [3072, 1024], P('tp')
Outputs:
- output 1: bfloat16 [8192, 1024], P(('dp', 'cp'))
- output 2: bfloat16 [8192, 8, 128], P(('dp', 'cp'), 'tp')
- output 3: bfloat16 [8192, 8, 128], P(('dp', 'cp'), 'tp')
All inputs are finite; a program needn't handle non-finite values.
Results may differ from a plain program's by a relative error of at most 0.0126497.
Values are sent between devices in bfloat16 or wider.
A program may use at most 768 MiB of HBM per device.

v0:
```python
import jax
import jax.numpy as jnp
from jax import lax
from jax.sharding import PartitionSpec as P

HEAD_DIM = 128
ROPE_BASE = 4000000
LN_EPS = 1e-5


def layer_norm(hidden, ln_gain):
    hidden_f = hidden.astype(jnp.float32)
    row_mean = jnp.mean(hidden_f, axis=-1, keepdims=True)
    centered = hidden_f - row_mean
    row_var = jnp.mean(centered * centered, axis=-1, keepdims=True)
    return (centered * lax.rsqrt(row_var + LN_EPS) * ln_gain.astype(jnp.float32)).astype(jnp.bfloat16)


def rotary(proj, positions):
    half_dim = HEAD_DIM // 2
    inv_freq = 1.0 / (ROPE_BASE ** (jnp.arange(0, HEAD_DIM, 2, dtype=jnp.float32) / HEAD_DIM))
    angles = positions.astype(jnp.float32)[:, None] * inv_freq[None, :]
    bcast_shape = (proj.shape[0],) + (1,) * (proj.ndim - 2) + (half_dim,)
    cosine = jnp.cos(angles).reshape(bcast_shape)
    sine_val = jnp.sin(angles).reshape(bcast_shape)
    paired = proj.astype(jnp.float32).reshape(proj.shape[:-1] + (half_dim, 2))
    even_part = paired[..., 0]
    odd_part = paired[..., 1]
    rotated = jnp.stack([even_part * cosine - odd_part * sine_val, odd_part * cosine + even_part * sine_val], axis=-1)
    return rotated.reshape(proj.shape).astype(jnp.bfloat16)


def attend_all(q_rot, k_all, v_all, my_block):
    tok_rows, kv_local, group_size, head_dim = q_rot.shape
    score_scale = head_dim ** -0.5
    query_pos = my_block * tok_rows + jnp.arange(tok_rows)

    def key_step(src_block, loop_state):
        row_max, row_sum, accum = loop_state
        k_block = lax.dynamic_index_in_dim(k_all, src_block, 0, keepdims=False)
        v_block = lax.dynamic_index_in_dim(v_all, src_block, 0, keepdims=False)
        scores = jnp.einsum('qkgd,tkd->kqgt', q_rot, k_block, preferred_element_type=jnp.float32) * score_scale
        key_pos = src_block * tok_rows + jnp.arange(tok_rows)
        allowed = (key_pos[None, :] <= query_pos[:, None])[None, :, None, :]
        scores = jnp.where(allowed, scores, -jnp.inf)
        new_max = jnp.maximum(row_max, jnp.max(scores, axis=-1))
        weights = jnp.exp(scores - new_max[..., None])
        factor = jnp.exp(row_max - new_max)
        new_sum = row_sum * factor + jnp.sum(weights, axis=-1)
        new_accum = accum * factor[..., None] + jnp.einsum('kqgt,tkd->kqgd', weights.astype(jnp.bfloat16), v_block, preferred_element_type=jnp.float32)
        return new_max, new_sum, new_accum

    state_shape = (kv_local, tok_rows, group_size)
    init_state = (jnp.full(state_shape, -jnp.inf, jnp.float32), jnp.zeros(state_shape, jnp.float32), jnp.zeros(state_shape + (head_dim,), jnp.float32))
    row_max, row_sum, accum = lax.fori_loop(0, my_block + 1, key_step, init_state)
    attn = (accum / row_sum[..., None]).astype(jnp.bfloat16)
    return jnp.transpose(attn, (1, 0, 2, 3)).reshape(tok_rows, kv_local * group_size * head_dim)


def solution(mesh):
    def local_layer(hidden, positions, ln_gain, w_q, w_k, w_v, w_o, w_gate, w_up, w_down):
        tok_rows = hidden.shape[0]
        kv_local = w_k.shape[1] // HEAD_DIM
        group_size = w_q.shape[1] // w_k.shape[1]
        my_block = lax.axis_index('cp')
        normed = layer_norm(hidden, ln_gain)
        q_proj = jnp.dot(normed, w_q, preferred_element_type=jnp.float32).astype(jnp.bfloat16)
        k_proj = jnp.dot(normed, w_k, preferred_element_type=jnp.float32).astype(jnp.bfloat16)
        v_cache = jnp.dot(normed, w_v, preferred_element_type=jnp.float32).astype(jnp.bfloat16).reshape(tok_rows, kv_local, HEAD_DIM)
        q_rot = rotary(q_proj.reshape(tok_rows, kv_local, group_size, HEAD_DIM), positions)
        k_cache = rotary(k_proj.reshape(tok_rows, kv_local, HEAD_DIM), positions)
        k_all = lax.all_gather(k_cache, 'cp')
        v_all = lax.all_gather(v_cache, 'cp')
        attn = attend_all(q_rot, k_all, v_all, my_block)
        attn_part = jnp.dot(attn, w_o, preferred_element_type=jnp.float32).astype(jnp.bfloat16)
        attn_sum = lax.psum(attn_part, 'tp')
        gate_proj = jnp.dot(normed, w_gate, preferred_element_type=jnp.float32).astype(jnp.bfloat16)
        up_proj = jnp.dot(normed, w_up, preferred_element_type=jnp.float32).astype(jnp.bfloat16)
        mlp_act = (jax.nn.silu(gate_proj.astype(jnp.float32)) * up_proj.astype(jnp.float32)).astype(jnp.bfloat16)
        mlp_part = jnp.dot(mlp_act, w_down, preferred_element_type=jnp.float32).astype(jnp.bfloat16)
        mlp_sum = lax.psum(mlp_part, 'tp')
        hidden_out = (hidden.astype(jnp.float32) + attn_sum.astype(jnp.float32) + mlp_sum.astype(jnp.float32)).astype(jnp.bfloat16)
        return hidden_out, k_cache, v_cache

    row_spec = P(('dp', 'cp'), None)
    col_spec = P(None, 'tp')
    cache_spec = P(('dp', 'cp'), 'tp', None)
    in_specs = (row_spec, P(('dp', 'cp')), P(None), col_spec, col_spec, col_spec, P('tp', None), col_spec, col_spec, P('tp', None))
    return jax.shard_map(local_layer, mesh=mesh, in_specs=in_specs, out_specs=(row_spec, cache_spec, cache_spec), check_vma=False)
```

profile of v0, /device:TPU:102, one launch (start us, length us, event | category | flops | bytes accessed | tf_op | source)
XLA Modules:
  0.0 319.8 jit_solution(9842303483256986817)
XLA Ops:
  7.3 0.8 convert_element_type.94
  8.1 2.0 convert_reduce_fusion
  10.1 0.7 fusion.21
  10.8 0.7 fusion.23
  11.6 1.3 copy-done.3
  12.9 0.8 convolution_convert_fusion.5
  13.7 1.0 copy.36
  14.8 2.3 fusion.34
  17.2 1.6 reshape.183
  18.8 1.0 multiply_cosine_fusion
  19.8 2.5 fusion.37
  22.2 1.1 multiply_subtract_fusion
  23.3 0.7 maximum_convert_fusion
  24.0 1.2 copy.33
  25.5 4.5 %fusion.33 = f32[1024,512]{0,1:T(8,128)} fusion(bf16[1024,1024]{1,0:T(8,128)(2,1)} %copy-done.3, bf16[1024,512]{1,0:T(8,128)(2,1)} %param.15), kind=kOutput, calls=%fused_computation.47 | convolution fusion | flops 1074790400 | bytes 5242880 | tf_op jit(solution)/shard_map/dot_general | solution.py:67
  30.0 3.5 %reshape.184 = f32[1024,2,2,64,2]{0,4,3,2,1:T(2,128)} reshape(f32[1024,512]{0,1:T(8,128)} %fusion.33) | data formatting | bytes 4194304 | tf_op jit(solution)/shard_map/convert_element_type | solution.py:26
  33.5 4.1 %fusion.36 = (f32[1024,2,2,64,1]{0,4,3,2,1:T(1,128)S(1)}, f32[1024,2,2,64,1]{0,4,3,2,1:T(1,128)S(1)}) fusion(f32[1024,2,2,64,2]{0,4,3,2,1:T(2,128)} %reshape.184), kind=kLoop, calls=%fused_computation.63 | loop fusion | bytes 4194304 | tf_op jit(solution)/shard_map/slice | solution.py:27
  37.6 1.7 subtract_convert_fusion
  39.3 1.4 pad_maximum_fusion
  40.7 2.1 copy.37
  42.8 5.0 %convolution_convert_fusion.2 = bf16[1024,768]{1,0:T(8,128)(2,1)} fusion(bf16[1024,1024]{1,0:T(8,128)(2,1)} %copy-done.3, bf16[1024,768]{1,0:T(8,128)(2,1)} %param.20), kind=kOutput, calls=%fused_computation.43 | convolution fusion | flops 1611399168 | bytes 5242880 | tf_op jit(solution)/shard_map/dot_general | solution.py:78
  47.7 8.3 %convolution_convert_fusion.1 = bf16[1024,1024]{1,0:T(8,128)(2,1)} fusion(bf16[768,1024]{1,0:T(8,128)(2,1)S(1)} %copy-done, bf16[1024,768]{1,0:T(8,128)(2,1)} %convolution_convert_fusion.2, bf16[1024,1024]{1,0:T(8,128)(2,1)} %copy-done.3, bf16[1024,768]{1,0:T(8,128)(2,1)} %param.19), kind=kOutput, calls=%fused_computation.42 | convolution fusion | flops 3229351936 | bytes 8912896 | tf_op jit(solution)/shard_map/dot_general | solution.py:80
  56.0 20.3 %all-gather.3.cloned.1.call-done = bf16[8,1024,2,128]{3,1,2,0:T(8,128)(2,1)} async-done(((bf16[1,1024,2,128]{3,1,2,0:T(8,128)(2,1)}), bf16[8,1024,2,128]{3,1,2,0:T(8,128)(2,1)}) %all-gather.3.cloned.1.call-update) | async-done | bytes 4194320 | tf_op jit(solution)/shard_map/all_gather | solution.py:72
  76.4 1.5 broadcast_in_dim.16
  77.9 116.8 %while.15 = (s32[]{:T(128)}, f32[2,1024,2]{1,2,0:T(2,128)S(1)}, f32[2,1024,2]{1,2,0:T(2,128)S(1)}, f32[2,1024,2,128]{3,1,2,0:T(8,128)}, s32[]{:T(128)}, /*index=...) while((s32[]{:T(128)}, f32[2,1024,2]{1,2,0:T(2,128)S(1)}, ...), condition=%wide.region_5.6_spmd.clone, body=%wide.region_2.5_spmd.clone.sunk | while | flops 2195728384 | bytes 77873400 | solution.py:55
  77.9 0.7 broadcast_compare_fusion.2
  78.5 4.0 %fusion.60 = (f32[2,1024,2]{1,2,0:T(2,128)S(1)}, f32[2,1024,1024,2]{2,1,3,0:T(8,128)S(1)}) fusion(pred[1024,1024]{0,1:T(8,128)(4,1)S(1)} %broadcast_compare_fusion.2, bf16[1024,2,2,128]{3,0,2,1:T(8,128)(2,1)S(1)} %get-tuple-element.239, bf16[8,1024,2,128]{3,1,2,0:T(8,128)(2,1)} %get-tuple-element.238, s32[]{:T(128)S(6)} %select_n.28), kind=kOutput, calls=%fused_computation.5.clone.1 | convolution fusion | flops 1086320640 | bytes 19415044 | tf_op jit(solution)/shard_map/while/body/qkgd,tkd->kqgt/dot_general | solution.py:42
  82.6 3.7 %fusion.61 = f32[2,1024,2]{1,2,0:T(2,128)S(1)} fusion(f32[2,1024,1024,2]{2,1,3,0:T(8,128)S(1)} %get-tuple-element.204, f32[2,1024,2]{1,2,0:T(2,128)S(1)} %max.5, pred[1024,1024]{0,1:T(8,128)(4,1)S(1)} %broadcast_compare_fusion.2), kind=kLoop, calls=%fused_computation.4.clone.1 | loop fusion | flops 16773120 | bytes 17858560 | tf_op jit(solution)/shard_map/while/body/reduce_sum | solution.py:49
  86.3 6.9 %multiply_add_fusion.6 = f32[2,1024,2,128]{3,1,2,0:T(8,128)S(1)} fusion(f32[2,1024,2,128]{3,1,2,0:T(8,128)S(1)} %copy-done.4, f32[2,1024,1024,2]{2,1,3,0:T(8,128)S(1)} %get-tuple-element.204, f32[2,1024,2]{1,2,0:T(2,128)S(1)} %max.5, pred[1024,1024]{0,1:T(8,128)(4,1)S(1)} %broadcast_compare_fusion.2, f32[2,1024,2]{1,2,0:T(2,128)S(1)} %get-tuple-element.206, ...), kind=kOutput, calls=%fused_computation.8.clone.1 | convolution fusion | flops 1091567616 | bytes 22577156 | tf_op jit(solution)/shard_map/while/body/kqgt,tkd->kqgd/dot_general | solution.py:50
  93.3 1.3 copy-done.5
  94.6 0.7 broadcast_compare_fusion.2
  95.2 4.0 %fusion.60 = (f32[2,1024,2]{1,2,0:T(2,128)S(1)}, f32[2,1024,1024,2]{2,1,3,0:T(8,128)S(1)}) fusion(pred[1024,1024]{0,1:T(8,128)(4,1)S(1)} %broadcast_compare_fusion.2, bf16[1024,2,2,128]{3,0,2,1:T(8,128)(2,1)S(1)} %get-tuple-element.239, bf16[8,1024,2,128]{3,1,2,0:T(8,128)(2,1)} %get-tuple-element.238, s32[]{:T(128)S(6)} %select_n.28), kind=kOutput, calls=%fused_computation.5.clone.1 | convolution fusion | flops 1086320640 | bytes 19415044 | tf_op jit(solution)/shard_map/while/body/qkgd,tkd->kqgt/dot_general | solution.py:42
  99.3 3.7 %fusion.61 = f32[2,1024,2]{1,2,0:T(2,128)S(1)} fusion(f32[2,1024,1024,2]{2,1,3,0:T(8,128)S(1)} %get-tuple-element.204, f32[2,1024,2]{1,2,0:T(2,128)S(1)} %max.5, pred[1024,1024]{0,1:T(8,128)(4,1)S(1)} %broadcast_compare_fusion.2), kind=kLoop, calls=%fused_computation.4.clone.1 | loop fusion | flops 16773120 | bytes 17858560 | tf_op jit(solution)/shard_map/while/body/reduce_sum | solution.py:49
  103.0 6.9 %multiply_add_fusion.6 = f32[2,1024,2,128]{3,1,2,0:T(8,128)S(1)} fusion(f32[2,1024,2,128]{3,1,2,0:T(8,128)S(1)} %copy-done.4, f32[2,1024,1024,2]{2,1,3,0:T(8,128)S(1)} %get-tuple-element.204, f32[2,1024,2]{1,2,0:T(2,128)S(1)} %max.5, pred[1024,1024]{0,1:T(8,128)(4,1)S(1)} %broadcast_compare_fusion.2, f32[2,1024,2]{1,2,0:T(2,128)S(1)} %get-tuple-element.206, ...), kind=kOutput, calls=%fused_computation.8.clone.1 | convolution fusion | flops 1091567616 | bytes 22577156 | tf_op jit(solution)/shard_map/while/body/kqgt,tkd->kqgd/dot_general | solution.py:50
  109.9 1.3 copy-done.5
  111.9 4.0 %fusion.60 = (f32[2,1024,2]{1,2,0:T(2,128)S(1)}, f32[2,1024,1024,2]{2,1,3,0:T(8,128)S(1)}) fusion(pred[1024,1024]{0,1:T(8,128)(4,1)S(1)} %broadcast_compare_fusion.2, bf16[1024,2,2,128]{3,0,2,1:T(8,128)(2,1)S(1)} %get-tuple-element.239, bf16[8,1024,2,128]{3,1,2,0:T(8,128)(2,1)} %get-tuple-element.238, s32[]{:T(128)S(6)} %select_n.28), kind=kOutput, calls=%fused_computation.5.clone.1 | convolution fusion | flops 1086320640 | bytes 19415044 | tf_op jit(solution)/shard_map/while/body/qkgd,tkd->kqgt/dot_general | solution.py:42
  116.0 3.7 %fusion.61 = f32[2,1024,2]{1,2,0:T(2,128)S(1)} fusion(f32[2,1024,1024,2]{2,1,3,0:T(8,128)S(1)} %get-tuple-element.204, f32[2,1024,2]{1,2,0:T(2,128)S(1)} %max.5, pred[1024,1024]{0,1:T(8,128)(4,1)S(1)} %broadcast_compare_fusion.2), kind=kLoop, calls=%fused_computation.4.clone.1 | loop fusion | flops 16773120 | bytes 17858560 | tf_op jit(solution)/shard_map/while/body/reduce_sum | solution.py:49
  119.7 6.9 %multiply_add_fusion.6 = f32[2,1024,2,128]{3,1,2,0:T(8,128)S(1)} fusion(f32[2,1024,2,128]{3,1,2,0:T(8,128)S(1)} %copy-done.4, f32[2,1024,1024,2]{2,1,3,0:T(8,128)S(1)} %get-tuple-element.204, f32[2,1024,2]{1,2,0:T(2,128)S(1)} %max.5, pred[1024,1024]{0,1:T(8,128)(4,1)S(1)} %broadcast_compare_fusion.2, f32[2,1024,2]{1,2,0:T(2,128)S(1)} %get-tuple-element.206, ...), kind=kOutput, calls=%fused_computation.8.clone.1 | convolution fusion | flops 1091567616 | bytes 22577156 | tf_op jit(solution)/shard_map/while/body/kqgt,tkd->kqgd/dot_general | solution.py:50
  126.6 1.3 copy-done.5
  127.9 0.7 broadcast_compare_fusion.2
  128.6 4.0 %fusion.60 = (f32[2,1024,2]{1,2,0:T(2,128)S(1)}, f32[2,1024,1024,2]{2,1,3,0:T(8,128)S(1)}) fusion(pred[1024,1024]{0,1:T(8,128)(4,1)S(1)} %broadcast_compare_fusion.2, bf16[1024,2,2,128]{3,0,2,1:T(8,128)(2,1)S(1)} %get-tuple-element.239, bf16[8,1024,2,128]{3,1,2,0:T(8,128)(2,1)} %get-tuple-element.238, s32[]{:T(128)S(6)} %select_n.28), kind=kOutput, calls=%fused_computation.5.clone.1 | convolution fusion | flops 1086320640 | bytes 19415044 | tf_op jit(solution)/shard_map/while/body/qkgd,tkd->kqgt/dot_general | solution.py:42
  132.7 3.7 %fusion.61 = f32[2,1024,2]{1,2,0:T(2,128)S(1)} fusion(f32[2,1024,1024,2]{2,1,3,0:T(8,128)S(1)} %get-tuple-element.204, f32[2,1024,2]{1,2,0:T(2,128)S(1)} %max.5, pred[1024,1024]{0,1:T(8,128)(4,1)S(1)} %broadcast_compare_fusion.2), kind=kLoop, calls=%fused_computation.4.clone.1 | loop fusion | flops 16773120 | bytes 17858560 | tf_op jit(solution)/shard_map/while/body/reduce_sum | solution.py:49
  136.4 6.9 %multiply_add_fusion.6 = f32[2,1024,2,128]{3,1,2,0:T(8,128)S(1)} fusion(f32[2,1024,2,128]{3,1,2,0:T(8,128)S(1)} %copy-done.4, f32[2,1024,1024,2]{2,1,3,0:T(8,128)S(1)} %get-tuple-element.204, f32[2,1024,2]{1,2,0:T(2,128)S(1)} %max.5, pred[1024,1024]{0,1:T(8,128)(4,1)S(1)} %broadcast_compare_fusion.2, f32[2,1024,2]{1,2,0:T(2,128)S(1)} %get-tuple-element.206, ...), kind=kOutput, calls=%fused_computation.8.clone.1 | convolution fusion | flops 1091567616 | bytes 22577156 | tf_op jit(solution)/shard_map/while/body/kqgt,tkd->kqgd/dot_general | solution.py:50
  143.3 1.3 copy-done.5
  145.3 4.0 %fusion.60 = (f32[2,1024,2]{1,2,0:T(2,128)S(1)}, f32[2,1024,1024,2]{2,1,3,0:T(8,128)S(1)}) fusion(pred[1024,1024]{0,1:T(8,128)(4,1)S(1)} %broadcast_compare_fusion.2, bf16[1024,2,2,128]{3,0,2,1:T(8,128)(2,1)S(1)} %get-tuple-element.239, bf16[8,1024,2,128]{3,1,2,0:T(8,128)(2,1)} %get-tuple-element.238, s32[]{:T(128)S(6)} %select_n.28), kind=kOutput, calls=%fused_computation.5.clone.1 | convolution fusion | flops 1086320640 | bytes 19415044 | tf_op jit(solution)/shard_map/while/body/qkgd,tkd->kqgt/dot_general | solution.py:42
  149.3 3.7 %fusion.61 = f32[2,1024,2]{1,2,0:T(2,128)S(1)} fusion(f32[2,1024,1024,2]{2,1,3,0:T(8,128)S(1)} %get-tuple-element.204, f32[2,1024,2]{1,2,0:T(2,128)S(1)} %max.5, pred[1024,1024]{0,1:T(8,128)(4,1)S(1)} %broadcast_compare_fusion.2), kind=kLoop, calls=%fused_computation.4.clone.1 | loop fusion | flops 16773120 | bytes 17858560 | tf_op jit(solution)/shard_map/while/body/reduce_sum | solution.py:49
  153.1 6.9 %multiply_add_fusion.6 = f32[2,1024,2,128]{3,1,2,0:T(8,128)S(1)} fusion(f32[2,1024,2,128]{3,1,2,0:T(8,128)S(1)} %copy-done.4, f32[2,1024,1024,2]{2,1,3,0:T(8,128)S(1)} %get-tuple-element.204, f32[2,1024,2]{1,2,0:T(2,128)S(1)} %max.5, pred[1024,1024]{0,1:T(8,128)(4,1)S(1)} %broadcast_compare_fusion.2, f32[2,1024,2]{1,2,0:T(2,128)S(1)} %get-tuple-element.206, ...), kind=kOutput, calls=%fused_computation.8.clone.1 | convolution fusion | flops 1091567616 | bytes 22577156 | tf_op jit(solution)/shard_map/while/body/kqgt,tkd->kqgd/dot_general | solution.py:50
  160.0 1.3 copy-done.5
  162.0 4.0 %fusion.60 = (f32[2,1024,2]{1,2,0:T(2,128)S(1)}, f32[2,1024,1024,2]{2,1,3,0:T(8,128)S(1)}) fusion(pred[1024,1024]{0,1:T(8,128)(4,1)S(1)} %broadcast_compare_fusion.2, bf16[1024,2,2,128]{3,0,2,1:T(8,128)(2,1)S(1)} %get-tuple-element.239, bf16[8,1024,2,128]{3,1,2,0:T(8,128)(2,1)} %get-tuple-element.238, s32[]{:T(128)S(6)} %select_n.28), kind=kOutput, calls=%fused_computation.5.clone.1 | convolution fusion | flops 1086320640 | bytes 19415044 | tf_op jit(solution)/shard_map/while/body/qkgd,tkd->kqgt/dot_general | solution.py:42
  166.0 3.7 %fusion.61 = f32[2,1024,2]{1,2,0:T(2,128)S(1)} fusion(f32[2,1024,1024,2]{2,1,3,0:T(8,128)S(1)} %get-tuple-element.204, f32[2,1024,2]{1,2,0:T(2,128)S(1)} %max.5, pred[1024,1024]{0,1:T(8,128)(4,1)S(1)} %broadcast_compare_fusion.2), kind=kLoop, calls=%fused_computation.4.clone.1 | loop fusion | flops 16773120 | bytes 17858560 | tf_op jit(solution)/shard_map/while/body/reduce_sum | solution.py:49
  169.7 6.9 %multiply_add_fusion.6 = f32[2,1024,2,128]{3,1,2,0:T(8,128)S(1)} fusion(f32[2,1024,2,128]{3,1,2,0:T(8,128)S(1)} %copy-done.4, f32[2,1024,1024,2]{2,1,3,0:T(8,128)S(1)} %get-tuple-element.204, f32[2,1024,2]{1,2,0:T(2,128)S(1)} %max.5, pred[1024,1024]{0,1:T(8,128)(4,1)S(1)} %broadcast_compare_fusion.2, f32[2,1024,2]{1,2,0:T(2,128)S(1)} %get-tuple-element.206, ...), kind=kOutput, calls=%fused_computation.8.clone.1 | convolution fusion | flops 1091567616 | bytes 22577156 | tf_op jit(solution)/shard_map/while/body/kqgt,tkd->kqgd/dot_general | solution.py:50
  176.7 1.3 copy-done.5
  178.7 4.0 %fusion.60 = (f32[2,1024,2]{1,2,0:T(2,128)S(1)}, f32[2,1024,1024,2]{2,1,3,0:T(8,128)S(1)}) fusion(pred[1024,1024]{0,1:T(8,128)(4,1)S(1)} %broadcast_compare_fusion.2, bf16[1024,2,2,128]{3,0,2,1:T(8,128)(2,1)S(1)} %get-tuple-element.239, bf16[8,1024,2,128]{3,1,2,0:T(8,128)(2,1)} %get-tuple-element.238, s32[]{:T(128)S(6)} %select_n.28), kind=kOutput, calls=%fused_computation.5.clone.1 | convolution fusion | flops 1086320640 | bytes 19415044 | tf_op jit(solution)/shard_map/while/body/qkgd,tkd->kqgt/dot_general | solution.py:42
  182.7 3.7 %fusion.61 = f32[2,1024,2]{1,2,0:T(2,128)S(1)} fusion(f32[2,1024,1024,2]{2,1,3,0:T(8,128)S(1)} %get-tuple-element.204, f32[2,1024,2]{1,2,0:T(2,128)S(1)} %max.5, pred[1024,1024]{0,1:T(8,128)(4,1)S(1)} %broadcast_compare_fusion.2), kind=kLoop, calls=%fused_computation.4.clone.1 | loop fusion | flops 16773120 | bytes 17858560 | tf_op jit(solution)/shard_map/while/body/reduce_sum | solution.py:49
  186.4 6.9 %multiply_add_fusion.6 = f32[2,1024,2,128]{3,1,2,0:T(8,128)S(1)} fusion(f32[2,1024,2,128]{3,1,2,0:T(8,128)S(1)} %copy-done.4, f32[2,1024,1024,2]{2,1,3,0:T(8,128)S(1)} %get-tuple-element.204, f32[2,1024,2]{1,2,0:T(2,128)S(1)} %max.5, pred[1024,1024]{0,1:T(8,128)(4,1)S(1)} %broadcast_compare_fusion.2, f32[2,1024,2]{1,2,0:T(2,128)S(1)} %get-tuple-element.206, ...), kind=kOutput, calls=%fused_computation.8.clone.1 | convolution fusion | flops 1091567616 | bytes 22577156 | tf_op jit(solution)/shard_map/while/body/kqgt,tkd->kqgd/dot_general | solution.py:50
  193.4 1.3 copy-done.5
  194.7 2.9 copy.38
  197.6 1.9 divide_convert_fusion
  199.6 2.6 convolution_convert_fusion
  202.3 1.0 copy-done.7
  203.2 1.1 copy.40
  204.3 1.9 copy.39
  206.2 101.3 %all-reduce.3.cloned.1.call-done = (bf16[1024,1024]{1,0:T(8,128)(2,1)}, bf16[1024,1024]{1,0:T(8,128)(2,1)}) async-done(((bf16[1024,1024]{1,0:T(8,128)(2,1)}, bf16[1024,1024]{1,0:T(8,128)(2,1)}), (bf16[1024,1024]{1,0:T(8,128)(2,1)}, bf16[1024,1024]{1,0:T(8,128)(2,1)})) %all-reduce.3.cloned.1.call-update) | async-done | bytes 4194320 | tf_op jit(solution)/shard_map/psum | solution.py:81
  307.5 5.8 %fusion.25 = bf16[1024,1024]{1,0:T(8,128)(2,1)} fusion(bf16[1024,1024]{1,0:T(8,128)(2,1)} %param.12, bf16[1024,1024]{1,0:T(8,128)(2,1)} %get-tuple-element.121, bf16[1024,1024]{1,0:T(8,128)(2,1)} %get-tuple-element.122), kind=kLoop, calls=%fused_computation.32 | loop fusion | flops 6291456 | bytes 8388608 | tf_op jit(solution)/shard_map/convert_element_type | solution.py:82
  (86 shorter events, 3.7 us)
Async XLA Ops:
  7.2 40.6 %copy-start = (bf16[768,1024]{1,0:T(8,128)(2,1)S(1)}, bf16[768,1024]{1,0:T(8,128)(2,1)}, u32[]{:S(2)}) copy-start(bf16[768,1024]{1,0:T(8,128)(2,1)} %param.21) | copy-start | bytes 4718596
  7.2 48.8 %all-gather.5.cloned.1.call-start = ((), (), s32[]{:S(2)}) async-start(), calls=%async_computation.1 | async-start | bytes 4718592 | tf_op jit(solution)/shard_map/all_gather | solution.py:73
  7.3 2.9 copy-start.2
  10.8 2.0 copy-start.12
  11.5 1.3 copy-start.3
  12.9 1.9 copy-start.10
  12.9 2.0 copy-start.9
  13.6 1.1 copy-start.6
  14.7 61.7 %all-gather.3.cloned.1.call-start = ((), (), s32[]{:S(2)}) async-start(), calls=%async_computation | async-start | bytes 4718592 | tf_op jit(solution)/shard_map/all_gather | solution.py:72
  25.2 282.3 %all-reduce.3.cloned.1.call-start = ((), (), s32[]{:S(2)}) async-start(), calls=%async_computation.2 | async-start | bytes 8388608 | tf_op jit(solution)/shard_map/psum | solution.py:81
  56.0 21.8 %copy-start.8 = (bf16[1024,2,2,128]{3,0,2,1:T(8,128)(2,1)S(1)}, bf16[1024,2,2,128]{3,0,2,1:T(8,128)(2,1)}, u32[]{:S(2)}) copy-start(bf16[1024,2,2,128]{3,0,2,1:T(8,128)(2,1)} %copy.37) | copy-start | bytes 3145732
  82.6 3.7 %copy-start.4 = (f32[2,1024,2,128]{3,1,2,0:T(8,128)S(1)}, f32[2,1024,2,128]{3,1,2,0:T(8,128)}, u32[]{:S(2)}) copy-start(f32[2,1024,2,128]{3,1,2,0:T(8,128)} %get-tuple-element.223) | copy-start | bytes 6291460 | tf_op jit(solution)/shard_map/while
  93.2 1.3 copy-start.5
  99.3 3.7 %copy-start.4 = (f32[2,1024,2,128]{3,1,2,0:T(8,128)S(1)}, f32[2,1024,2,128]{3,1,2,0:T(8,128)}, u32[]{:S(2)}) copy-start(f32[2,1024,2,128]{3,1,2,0:T(8,128)} %get-tuple-element.223) | copy-start | bytes 6291460 | tf_op jit(solution)/shard_map/while
  109.9 1.3 copy-start.5
  116.0 3.7 %copy-start.4 = (f32[2,1024,2,128]{3,1,2,0:T(8,128)S(1)}, f32[2,1024,2,128]{3,1,2,0:T(8,128)}, u32[]{:S(2)}) copy-start(f32[2,1024,2,128]{3,1,2,0:T(8,128)} %get-tuple-element.223) | copy-start | bytes 6291460 | tf_op jit(solution)/shard_map/while
  126.6 1.3 copy-start.5
  132.6 3.7 %copy-start.4 = (f32[2,1024,2,128]{3,1,2,0:T(8,128)S(1)}, f32[2,1024,2,128]{3,1,2,0:T(8,128)}, u32[]{:S(2)}) copy-start(f32[2,1024,2,128]{3,1,2,0:T(8,128)} %get-tuple-element.223) | copy-start | bytes 6291460 | tf_op jit(solution)/shard_map/while
  143.3 1.3 copy-start.5
  149.3 3.7 %copy-start.4 = (f32[2,1024,2,128]{3,1,2,0:T(8,128)S(1)}, f32[2,1024,2,128]{3,1,2,0:T(8,128)}, u32[]{:S(2)}) copy-start(f32[2,1024,2,128]{3,1,2,0:T(8,128)} %get-tuple-element.223) | copy-start | bytes 6291460 | tf_op jit(solution)/shard_map/while
  160.0 1.3 copy-start.5
  166.0 3.7 %copy-start.4 = (f32[2,1024,2,128]{3,1,2,0:T(8,128)S(1)}, f32[2,1024,2,128]{3,1,2,0:T(8,128)}, u32[]{:S(2)}) copy-start(f32[2,1024,2,128]{3,1,2,0:T(8,128)} %get-tuple-element.223) | copy-start | bytes 6291460 | tf_op jit(solution)/shard_map/while
  176.7 1.3 copy-start.5
  182.7 3.7 %copy-start.4 = (f32[2,1024,2,128]{3,1,2,0:T(8,128)S(1)}, f32[2,1024,2,128]{3,1,2,0:T(8,128)}, u32[]{:S(2)}) copy-start(f32[2,1024,2,128]{3,1,2,0:T(8,128)} %get-tuple-element.223) | copy-start | bytes 6291460 | tf_op jit(solution)/shard_map/while
  193.4 1.3 copy-start.5
  197.6 1.9 copy-start.11
  202.2 1.0 copy-start.7
  307.5 5.8 %copy-start.1 = (bf16[768,1024]{1,0:T(8,128)(2,1)S(1)}, bf16[768,1024]{1,0:T(8,128)(2,1)}, u32[]{:S(2)}) copy-start(bf16[768,1024]{1,0:T(8,128)(2,1)} %param.21) | copy-start | bytes 4718596
Sparse Core Ops, SparseCore 0:
  14.8 30.0 all-gather.4
  47.2 29.1 all-gather.2
  202.4 105.0 all-reduce.2
where the time goes:
time: 322 us; the launch traced here: 320 us
  waiting for transfers between devices  122 us (38%)
  matrix products  100 us (31%)
  other arithmetic  48.2 us (15%)
  local copies, waits for them, and re-layouts  34.8 us (11%)
  between operations  14 us (4%)
    psum x1, waiting for transfers between devices, local_layer(): mlp_sum = lax.psum(mlp_part, 'tp')  101 us
    dot_general x7, matrix products, key_step(): jnp.einsum('kqgt,tkd->kqgd', weights.astype(jnp.bfloat16), v_block, prefe...  48.5 us
    dot_general x7, matrix products, key_step(): jnp.einsum('qkgd,tkd->kqgt', q_rot, k_block, preferred_element_type=jnp.f...  28.1 us
    reduce_sum x7, other arithmetic, key_step(): new_sum = row_sum * factor + jnp.sum(weights, axis=-1)  25.6 us
    all_gather x1, waiting for transfers between devices, local_layer(): k_all = lax.all_gather(k_cache, 'cp')  20.3 us
    while x35, local copies, waits for them, and re-layouts  9.18 us
    dot_general x1, matrix products, local_layer(): jnp.dot(mlp_act, w_down, preferred_element_type=jnp.float32)  8.29 us
    unnamed x25, local copies, waits for them, and re-layouts  7.43 us
  transfers between devices with their start and end apart: 3, of which 2 were waited for; matrix products, arithmetic and copies ran while one was open for 14% of the time, Pallas kernels for 0%

commit v1 on v0

v1 whole, which is shorter than its diff:
```python
import functools

import jax
import jax.numpy as jnp
from jax import lax
from jax.experimental import pallas as pl
from jax.experimental.pallas import tpu as pltpu
from jax.sharding import PartitionSpec as P

HEAD_DIM = 128
ROPE_BASE = 4000000
LN_EPS = 1e-5
EXP2_SCALE = (HEAD_DIM ** -0.5) * 1.4426950408889634
MESH = pl.DeviceIdType.MESH
BF16 = jnp.bfloat16
F32 = jnp.float32


def rope_tables(positions):
    pair = jnp.repeat(jnp.arange(0, HEAD_DIM, 2, dtype=F32), 2)
    inv_freq = 1.0 / (ROPE_BASE ** (pair / HEAD_DIM))
    angles = positions.astype(F32)[:, None] * inv_freq[None, :]
    sign = jnp.where(jnp.arange(HEAD_DIM) % 2 == 0, -1.0, 1.0).astype(F32)
    return jnp.cos(angles), jnp.sin(angles) * sign[None, :]


def proj_kernel(hid_ref, cos_ref, sin_ref, gain_ref, wq_ref, wk_ref, wv_ref, h_ref, kvx_ref, kc_ref, vc_ref):
    x = hid_ref[...].astype(F32)
    mean = jnp.mean(x, axis=-1, keepdims=True)
    cent = x - mean
    var = jnp.mean(cent * cent, axis=-1, keepdims=True)
    h = (cent * lax.rsqrt(var + LN_EPS) * gain_ref[...].astype(F32)).astype(BF16)
    h_ref[...] = h
    cos, sin = cos_ref[...], sin_ref[...]
    even = lax.broadcasted_iota(jnp.int32, cos.shape, 1) % 2 == 0

    def rope(col):
        u = col.astype(BF16).astype(F32)
        swapped = jnp.where(even, pltpu.roll(u, HEAD_DIM - 1, 1), pltpu.roll(u, 1, 1))
        return (u * cos + swapped * sin).astype(BF16)

    q = jnp.dot(h, wq_ref[...], preferred_element_type=F32)
    k = jnp.dot(h, wk_ref[...], preferred_element_type=F32)
    v = jnp.dot(h, wv_ref[...], preferred_element_type=F32).astype(BF16)
    for g in range(2):
        kg = rope(k[:, g * HEAD_DIM:(g + 1) * HEAD_DIM])
        vg = v[:, g * HEAD_DIM:(g + 1) * HEAD_DIM]
        kvx_ref[g, 0] = kg
        kvx_ref[g, 1] = vg
        kc_ref[:, g * HEAD_DIM:(g + 1) * HEAD_DIM] = kg
        vc_ref[:, g * HEAD_DIM:(g + 1) * HEAD_DIM] = vg
        for j in range(2):
            lo = (2 * g + j) * HEAD_DIM
            kvx_ref[g, 2 + j] = rope(q[:, lo:lo + HEAD_DIM])


def project(hidden, cos, sin, gain, w_q, w_k, w_v):
    rows, width = hidden.shape
    tile = 256
    full = lambda a: pl.BlockSpec(a.shape, lambda i: (0, 0))
    return pl.pallas_call(
        proj_kernel,
        grid=(rows // tile,),
        in_specs=[
            pl.BlockSpec((tile, width), lambda i: (i, 0)),
            pl.BlockSpec((tile, HEAD_DIM), lambda i: (i, 0)),
            pl.BlockSpec((tile, HEAD_DIM), lambda i: (i, 0)),
            full(gain), full(w_q), full(w_k), full(w_v),
        ],
        out_specs=[
            pl.BlockSpec((tile, width), lambda i: (i, 0)),
            pl.BlockSpec((2, 4, tile, HEAD_DIM), lambda i: (0, 0, i, 0)),
            pl.BlockSpec((tile, 2 * HEAD_DIM), lambda i: (i, 0)),
            pl.BlockSpec((tile, 2 * HEAD_DIM), lambda i: (i, 0)),
        ],
        out_shape=[
            jax.ShapeDtypeStruct((rows, width), BF16),
            jax.ShapeDtypeStruct((2, 4, rows, HEAD_DIM), BF16),
            jax.ShapeDtypeStruct((rows, 2 * HEAD_DIM), BF16),
            jax.ShapeDtypeStruct((rows, 2 * HEAD_DIM), BF16),
        ],
        compiler_params=pltpu.CompilerParams(vmem_limit_bytes=40 << 20),
        name='proj',
    )(hidden, cos, sin, gain, w_q, w_k, w_v)


def layer_kernel(h_hbm, kvx_hbm, hid_hbm, wg_hbm, wu_hbm, wd_hbm, wo_hbm, out_hbm,
                 kvbuf, qbuf, acc, mbuf, lbuf, h, wg, wu, wd, wo, act, part, resid,
                 oown, osend, orecv, pbuf, rs1, sum2, rs2, xbuf,
                 load_sem, kvs_sem, kvr_sem, dds_sem, ddr_sem, ys_sem, yr_sem, out_sem):
    cp = lax.axis_index('cp')
    y = lax.axis_index('tp')
    x = cp // 2
    c = cp % 2
    partner = 2 * x + 1 - c
    right = ((x + 1) % 4) * 2 + c
    left = ((x + 3) % 4) * 2 + c
    y1 = y + 1 - 2 * (y % 2)
    y2 = 3 - y
    rows = h_hbm.shape[0]
    half_rows = rows // 2
    quarter = half_rows // 4
    sub = 256

    barrier = pltpu.get_barrier_semaphore()
    for dev in ({'cp': partner}, {'cp': right}, {'cp': left}, {'tp': y1}, {'tp': y2}):
        pl.semaphore_signal(barrier, inc=1, device_id=dev, device_id_type=MESH)

    own_kv = pltpu.make_async_copy(kvx_hbm.at[c, pl.ds(0, 2)], kvbuf.at[2 * x + c], load_sem.at[0])
    own_q = pltpu.make_async_copy(kvx_hbm.at[c, pl.ds(2, 2)], qbuf.at[c], load_sem.at[1])
    own_kv.start()
    own_q.start()
    loads = []
    for i, (src, dst) in enumerate(((h_hbm, h), (wg_hbm, wg), (wu_hbm, wu), (wd_hbm, wd), (wo_hbm, wo))):
        loads.append(pltpu.make_async_copy(src, dst, load_sem.at[2 + i]))
    for b in range(2):
        loads.append(pltpu.make_async_copy(
            hid_hbm.at[pl.ds(b * half_rows + y * quarter, quarter)], resid.at[b], load_sem.at[7 + b]))
    pl.semaphore_wait(barrier, 5)

    def remote(src, dst, ss, rsem, dev):
        return pltpu.make_async_remote_copy(src_ref=src, dst_ref=dst, send_sem=ss, recv_sem=rsem,
                                            device_id=dev, device_id_type=MESH)

    dd_kv = remote(kvx_hbm.at[1 - c, pl.ds(0, 2)], kvbuf.at[2 * x + c], dds_sem.at[0], ddr_sem.at[0], {'cp': partner})
    dd_q = remote(kvx_hbm.at[1 - c, pl.ds(2, 2)], qbuf.at[c], dds_sem.at[1], ddr_sem.at[1], {'cp': partner})
    dd_kv.start()
    dd_q.start()

    def kv_copy(ch, slot, dev):
        return remote(kvbuf.at[ch], kvbuf.at[ch], kvs_sem.at[slot], kvr_sem.at[ch], {'cp': dev})

    own_ch = 2 * x + c
    oth_ch = 2 * x + 1 - c
    own_kv.wait()

    @pl.when(x < 3)
    def _():
        kv_copy(own_ch, 0, right).start()

    @pl.when(x == 0)
    def _():
        kv_copy(own_ch, 1, left).start()

    for l in loads:
        l.start()
    loads[0].wait()
    loads[1].wait()
    loads[2].wait()
    loads[3].wait()

    def mlp(i, carry):
        rs = pl.ds(pl.multiple_of(i * sub, sub), sub)
        hh = h[rs, :]
        gate = jnp.dot(hh, wg[...], preferred_element_type=F32).astype(BF16).astype(F32)
        up = jnp.dot(hh, wu[...], preferred_element_type=F32).astype(BF16).astype(F32)
        a = (gate * (1.0 / (1.0 + jnp.exp(-gate))) * up).astype(BF16)
        part[rs, :] = jnp.dot(a, wd[...], preferred_element_type=F32)
        return carry

    lax.fori_loop(0, rows // sub, mlp, 0)

    remote(kvx_hbm.at[1 - c, pl.ds(0, 2)], kvbuf.at[oth_ch], dds_sem.at[0], ddr_sem.at[0], {'cp': partner}).wait_recv()
    remote(kvx_hbm.at[1 - c, pl.ds(2, 2)], qbuf.at[1 - c], dds_sem.at[1], ddr_sem.at[1], {'cp': partner}).wait_recv()
    own_q.wait()

    @pl.when(x < 3)
    def _():
        kv_copy(oth_ch, 2, right).start()

    @pl.when(x == 0)
    def _():
        kv_copy(oth_ch, 3, left).start()

    def lane_sum(p):
        s = p[:, :HEAD_DIM]
        for j in range(1, p.shape[1] // HEAD_DIM):
            s = s + p[:, j * HEAD_DIM:(j + 1) * HEAD_DIM]
        return s

    def qk(qv, kv):
        return lax.dot_general(qv, kv, (((1,), (1,)), ((), ())), preferred_element_type=F32)

    k0, k1, v0, v1 = (kvbuf.at[2 * x, 0], kvbuf.at[2 * x + 1, 0], kvbuf.at[2 * x, 1], kvbuf.at[2 * x + 1, 1])
    tri = (lax.broadcasted_iota(jnp.int32, (sub, sub), 1) <= lax.broadcasted_iota(jnp.int32, (sub, sub), 0))
    groups = rows // sub

    def diag_scores(r, g):
        half, off = r // groups, (r % groups) * sub
        qv = qbuf[half, g, pl.ds(off, sub), :]
        pieces = []
        if half == 1:
            pieces.append(qk(qv, k0[...]))
        kk = k0 if half == 0 else k1
        if off:
            pieces.append(qk(qv, kk[pl.ds(0, off), :]))
        pieces.append(jnp.where(tri, qk(qv, kk[pl.ds(off, sub), :]), -jnp.inf))
        return pieces[0] if len(pieces) == 1 else jnp.concatenate(pieces, axis=1)

    def diag_soft(r, g, s):
        half, off = r // groups, (r % groups) * sub
        rs = pl.ds(off, sub)
        mx = jnp.max(s, axis=1, keepdims=True)
        p = jnp.exp2((s - mx) * EXP2_SCALE)
        pb = p.astype(BF16)
        if half == 0:
            o = jnp.dot(pb, v0[pl.ds(0, off + sub), :], preferred_element_type=F32)
        else:
            o = jnp.dot(pb[:, :rows], v0[...], preferred_element_type=F32)
            o = o + jnp.dot(pb[:, rows:], v1[pl.ds(0, off + sub), :], preferred_element_type=F32)
        mbuf[g, half, rs, :] = jnp.broadcast_to(mx, (sub, HEAD_DIM))
        lbuf[g, half, rs, :] = lane_sum(p)
        acc[g, half, rs, :] = o

    items = [(r, g) for r in range(2 * groups) for g in range(2)]
    s_now = diag_scores(*items[0])
    for i, it in enumerate(items):
        s_next = diag_scores(*items[i + 1]) if i + 1 < len(items) else None
        diag_soft(*it, s_now)
        s_now = s_next

    for l in loads[4:]:
        l.wait()

    def attend(ch, b):
        kk, vv = kvbuf.at[ch, 0], kvbuf.at[ch, 1]
        its = [(g, half, pl.ds(pl.multiple_of(b * half_rows + j * sub, sub), sub))
               for half in range(2) for j in range(half_rows // sub) for g in range(2)]

        def scores(it):
            g, half, rs = it
            return qk(qbuf[half, g, rs, :], kk[...])

        s = scores(its[0])
        for i, it in enumerate(its):
            s_n = scores(its[i + 1]) if i + 1 < len(its) else None
            g, half, rs = it
            m_old = mbuf[g, half, rs, :]
            m_new = jnp.maximum(m_old, jnp.max(s, axis=1, keepdims=True))
            alpha = jnp.exp2((m_old - m_new) * EXP2_SCALE)
            p = jnp.exp2((s - m_new[:, :1]) * EXP2_SCALE)
            lbuf[g, half, rs, :] = lbuf[g, half, rs, :] * alpha + lane_sum(p)
            acc[g, half, rs, :] = acc[g, half, rs, :] * alpha + jnp.dot(
                p.astype(BF16), vv[...], preferred_element_type=F32)
            mbuf[g, half, rs, :] = m_new
            s = s_n

    first = (y1, y2)
    second = (y2, y1)

    def y_copy(src, dst, b, i, dev):
        return remote(src, dst, ys_sem.at[b, i], yr_sem.at[b, i], {'tp': dev})

    def rs1_copy(b, hf, slot):
        dev = first[hf]
        far = (3 - dev) if hf == 0 else (dev + 1 - 2 * (dev % 2))
        tile = dev if slot == 0 else far
        return y_copy(pbuf.at[b, tile, hf], rs1.at[b, hf, slot], b, 2 * hf + slot, dev)

    def rs2_copy(b, hf):
        return y_copy(sum2.at[b, hf], rs2.at[b, hf], b, 4 + hf, second[hf])

    def ag1_copy(b, hf):
        return y_copy(xbuf.at[b, y, hf], xbuf.at[b, y, hf], b, 6 + hf, second[hf])

    def ag1_wait(b, hf):
        t = second[hf]
        y_copy(xbuf.at[b, t, hf], xbuf.at[b, t, hf], b, 6 + hf, t).wait_recv()

    def ag2_copy(b, hf, slot):
        t = y if slot == 0 else second[hf]
        return y_copy(xbuf.at[b, t, hf], xbuf.at[b, t, hf], b, 8 + 2 * hf + slot, first[hf])

    def ag2_wait(b, hf, slot):
        dev = first[hf]
        far = (3 - dev) if hf == 0 else (dev + 1 - 2 * (dev % 2))
        t = dev if slot == 0 else far
        y_copy(xbuf.at[b, t, hf], xbuf.at[b, t, hf], b, 8 + 2 * hf + slot, dev).wait_recv()

    def o_copy(b):
        return remote(osend.at[b], orecv.at[b], dds_sem.at[2 + b], ddr_sem.at[2 + b], {'cp': partner})

    cols = (0, 512)

    def finish(b):
        base = b * half_rows

        def norm(half, j):
            rs = pl.ds(pl.multiple_of(base + j * quarter, quarter), quarter)
            out = []
            for g in range(2):
                den = jnp.sum(lbuf[g, half, rs, :], axis=1, keepdims=True)
                out.append((acc[g, half, rs, :] / den).astype(BF16))
            return jnp.concatenate(out, axis=1)

        def send_norm(j, carry):
            osend[b, pl.ds(pl.multiple_of(j * quarter, quarter), quarter), :] = norm(1 - c, j)
            return carry

        lax.fori_loop(0, 4, send_norm, 0)
        o_copy(b).start()
        wo_own = wo.at[pl.ds(pl.multiple_of(c * 2 * HEAD_DIM, 2 * HEAD_DIM), 2 * HEAD_DIM), :]
        wo_oth = wo.at[pl.ds(pl.multiple_of((1 - c) * 2 * HEAD_DIM, 2 * HEAD_DIM), 2 * HEAD_DIM), :]

        def own_part(j, carry):
            rs = pl.ds(pl.multiple_of(base + j * quarter, quarter), quarter)
            part[rs, :] = part[rs, :] + jnp.dot(norm(c, j), wo_own[...], preferred_element_type=F32)
            return carry

        lax.fori_loop(0, 4, own_part, 0)
        o_copy(b).wait_recv()

        def oth_part(j, carry):
            rs = pl.ds(pl.multiple_of(base + j * quarter, quarter), quarter)
            o = orecv[b, pl.ds(pl.multiple_of(j * quarter, quarter), quarter), :]
            tot = part[rs, :] + jnp.dot(o, wo_oth[...], preferred_element_type=F32)
            for hf in range(2):
                pbuf[b, j, hf] = tot[:, cols[hf]:cols[hf] + 512].astype(BF16)
            return carry

        lax.fori_loop(0, 4, oth_part, 0)
        for hf in range(2):
            for slot in range(2):
                rs1_copy(b, hf, 1 - slot).start()

    def step1(b):
        for hf in range(2):
            rs1_copy(b, hf, 1).wait_recv()
            other = second[hf]
            sum2[b, hf] = (pbuf[b, other, hf].astype(F32) + rs1[b, hf, 1].astype(F32)).astype(BF16)
            rs2_copy(b, hf).start()

    def step2(b):
        for hf in range(2):
            rs1_copy(b, hf, 0).wait_recv()
            rs2_copy(b, hf).wait_recv()
            tot = pbuf[b, y, hf].astype(F32) + rs1[b, hf, 0].astype(F32) + rs2[b, hf].astype(F32)
            tot = tot + resid[b, :, cols[hf]:cols[hf] + 512].astype(F32)
            xbuf[b, y, hf] = tot.astype(BF16)
            ag1_copy(b, hf).start()
            ag2_copy(b, hf, 0).start()

    def step3(b):
        for hf in range(2):
            ag1_wait(b, hf)
            ag2_copy(b, hf, 1).start()

    def out_copy(b, t, hf):
        return pltpu.make_async_copy(
            xbuf.at[b, t, hf],
            out_hbm.at[pl.ds(b * half_rows + t * quarter, quarter), pl.ds(cols[hf], 512)],
            out_sem.at[b, t, hf])

    def step4(b):
        for hf in range(2):
            for slot in range(2):
                ag2_wait(b, hf, slot)
        for t in range(4):
            for hf in range(2):
                out_copy(b, t, hf).start()

    n = 2 * x

    def chunk_of(s):
        first_half = s // 2
        par = s % 2
        near = 2 * (x - 1 - first_half) + (c + par - 2 * c * par)
        mix_half = c + first_half - 2 * c * first_half
        mixed = 4 - 4 * par + mix_half
        late = 2 + (c + par - 2 * c * par)
        three = jnp.where(s < 4, mixed, late)
        return jnp.where(x == 3, three, near)

    steps = 4 * x + 4 * (1 - (x + 3) // 4)

    def loop(t, carry):
        lead = steps - 4
        tail = t - lead
        in_tail = t >= lead
        s = jnp.where(in_tail, n - 2 + tail % 2, t // 2)
        b = jnp.where(in_tail, tail // 2, t % 2)

        @pl.when(x > 0)
        def _():
            ch = chunk_of(s)

            @pl.when(b == 0)
            def _():
                kv_copy(ch, 0, right).wait_recv()

                @pl.when(jnp.logical_and(x == 2, s < 2))
                def _():
                    kv_copy(ch, 1 + 2 * (s % 2), right).start()

                @pl.when(jnp.logical_and(x == 3, jnp.logical_and(s < 4, s % 2 == 1)))
                def _():
                    kv_copy(ch, s // 2, left).start()

            attend(ch, b)

        @pl.when(t == steps - 3)
        def _():
            finish(0)

        @pl.when(t == steps - 2)
        def _():
            step1(0)

        @pl.when(t == steps - 1)
        def _():
            step2(0)
        return carry

    lax.fori_loop(0, steps, loop, 0)
    finish(1)
    step3(0)
    step1(1)
    step4(0)
    step2(1)
    step3(1)
    step4(1)

    dd_kv.wait_send()
    dd_q.wait_send()

    @pl.when(x < 3)
    def _():
        kv_copy(own_ch, 0, right).wait_send()
        kv_copy(oth_ch, 2, right).wait_send()

    @pl.when(x == 0)
    def _():
        kv_copy(own_ch, 1, left).wait_send()
        kv_copy(oth_ch, 3, left).wait_send()

    @pl.when(x == 2)
    def _():
        kv_copy(own_ch, 1, right).wait_send()
        kv_copy(own_ch, 3, right).wait_send()

    @pl.when(x == 3)
    def _():
        kv_copy(own_ch, 0, left).wait_send()
        kv_copy(own_ch, 1, left).wait_send()

    for b in range(2):
        o_copy(b).wait_send()
        for hf in range(2):
            rs2_copy(b, hf).wait_send()
            ag1_copy(b, hf).wait_send()
            for slot in range(2):
                rs1_copy(b, hf, slot).wait_send()
                ag2_copy(b, hf, slot).wait_send()
        for t in range(4):
            for hf in range(2):
                out_copy(b, t, hf).wait()


def layer(h, kvx, hidden, w_gate, w_up, w_down, w_o):
    rows, width = h.shape
    ff = w_gate.shape[1]
    hr = rows // 2
    qr = hr // 4
    hw = width // 2
    anyspec = pl.BlockSpec(memory_space=pl.ANY)
    vm = pltpu.VMEM
    return pl.pallas_call(
        layer_kernel,
        in_specs=[anyspec] * 7,
        out_specs=anyspec,
        out_shape=jax.ShapeDtypeStruct((rows, width), BF16),
        scratch_shapes=[
            vm((8, 2, rows, HEAD_DIM), BF16),
            vm((2, 2, rows, HEAD_DIM), BF16),
            vm((2, 2, rows, HEAD_DIM), F32),
            vm((2, 2, rows, HEAD_DIM), F32),
            vm((2, 2, rows, HEAD_DIM), F32),
            vm((rows, width), BF16),
            vm((width, ff), BF16), vm((width, ff), BF16), vm((ff, width), BF16),
            vm(w_o.shape, BF16),
            vm((8, 128), BF16),
            vm((rows, width), F32),
            vm((2, qr, width), BF16),
            vm((8, 128), BF16),
            vm((2, hr, 2 * HEAD_DIM), BF16),
            vm((2, hr, 2 * HEAD_DIM), BF16),
            vm((2, 4, 2, qr, hw), BF16),
            vm((2, 2, 2, qr, hw), BF16),
            vm((2, 2, qr, hw), BF16),
            vm((2, 2, qr, hw), BF16),
            vm((2, 4, 2, qr, hw), BF16),
            pltpu.SemaphoreType.DMA((9,)),
            pltpu.SemaphoreType.DMA((4,)),
            pltpu.SemaphoreType.DMA((8,)),
            pltpu.SemaphoreType.DMA((4,)),
            pltpu.SemaphoreType.DMA((4,)),
            pltpu.SemaphoreType.DMA((2, 12)),
            pltpu.SemaphoreType.DMA((2, 12)),
            pltpu.SemaphoreType.DMA((2, 4, 2)),
        ],
        compiler_params=pltpu.CompilerParams(collective_id=0, has_side_effects=True, vmem_limit_bytes=60 << 20),
        name='layer',
    )(h, kvx, hidden, w_gate, w_up, w_down, w_o)


def solution(mesh):
    def local_layer(hidden, positions, ln_gain, w_q, w_k, w_v, w_o, w_gate, w_up, w_down):
        rows = hidden.shape[0]
        kv_local = w_k.shape[1] // HEAD_DIM
        cos, sin = rope_tables(positions)
        h, kvx, kc, vc = project(hidden, cos, sin, ln_gain[None, :], w_q, w_k, w_v)
        out = layer(h, kvx, hidden, w_gate, w_up, w_down, w_o)
        return out, kc.reshape(rows, kv_local, HEAD_DIM), vc.reshape(rows, kv_local, HEAD_DIM)

    row_spec = P(('dp', 'cp'), None)
    col_spec = P(None, 'tp')
    cache_spec = P(('dp', 'cp'), 'tp', None)
    in_specs = (row_spec, P(('dp', 'cp')), P(None), col_spec, col_spec, col_spec, P('tp', None), col_spec, col_spec, P('tp', None))
    return jax.shard_map(local_layer, mesh=mesh, in_specs=in_specs, out_specs=(row_spec, cache_spec, cache_spec), check_vma=False)
```

time: 322 us -> 121 us (0.38)
  waiting for transfers between devices: 122 us -> 0 us
  Pallas kernels: 0 us -> 104 us
  matrix products: 100 us -> 0 us
  other arithmetic: 48.2 us -> 2.61 us
  local copies, waits for them, and re-layouts: 34.8 us -> 13.4 us
  between operations: 14 us -> 0.69 us
    pallas_call x0 -> x2, Pallas kernels: none -> 104 us  [the longest x1 99.4 us: layer(): pl.pallas_call(layer_kernel, in_specs=[anyspec] * 7, out_specs=anyspec, o...]
    psum x1 -> x0, waiting for transfers between devices: 101 us -> none  [local_layer(): mlp_sum = lax.psum(mlp_part, 'tp')]
    dot_general x20 -> x0, matrix products: 100 us -> none  [the longest x7 48.5 us: key_step(): jnp.einsum('kqgt,tkd->kqgd', weights.astype(jnp.bfloat16), v_block, prefe...]
    reduce_sum x9 -> x0, other arithmetic: 28.3 us -> none  [the longest x7 25.6 us: key_step(): new_sum = row_sum * factor + jnp.sum(weights, axis=-1)]
    all_gather x2 -> x0, waiting for transfers between devices: 20.3 us -> none  [the longest x1 20.3 us: local_layer(): k_all = lax.all_gather(k_cache, 'cp')]
    while x36 -> x0, local copies, waits for them, and re-layouts: 12.1 us -> none
    convert_element_type x6 -> x1, other arithmetic: 9.9 us -> 0.69 us  [rope_tables(): angles = positions.astype(F32)[:, None] * inv_freq[None, :]]
    slice x2 -> x0, local copies, waits for them, and re-layouts: 6.57 us -> none  [rotary(): even_part = paired[..., 0]]
  transfers between devices with their start and end apart: 3 -> 0, of which waited for: 2 -> 0; matrix products, arithmetic and copies ran while one was open for 14% -> 0% of each run, Pallas kernels for 0% -> 0%
where the time goes in v1:
time: 121 us
  Pallas kernels  104 us (86%)
  local copies, waits for them, and re-layouts  13.4 us (11%)
  other arithmetic  2.61 us (2%)
    pallas_call x1, Pallas kernels, layer(): pl.pallas_call(layer_kernel, in_specs=[anyspec] * 7, out_specs=anyspec, o...  99.4 us
    unnamed x13, local copies, waits for them, and re-layouts  10.6 us
    pallas_call x1, Pallas kernels, project(): pl.pallas_call(proj_kernel, grid=(rows // tile,), in_specs=[pl.BlockSpec(...  4.57 us

profile of v1, /device:TPU:102, one launch (start us, length us, event | category | flops | bytes accessed | tf_op | source)
XLA Modules:
  0.0 120.7 jit_solution(13299289274567522340)
XLA Ops:
  0.7 0.7 convert_element_type.3
  1.3 0.7 broadcast_in_dim.17.gain_ref
  2.0 0.1 broadcast_in_dim.15
  2.1 0.1 pow.13
  2.2 1.9 %fusion = (f32[1024,128]{1,0:T(8,128)S(1)}, f32[1024,128]{1,0:T(8,128)S(1)}) fusion(f32[128]{0:T(128)S(1)} %compare_select_fusion, f32[128]{0:T(128)S(1)} %pow.13, f32[1024]{0:T(1024)S(1)} %convert_element_type.3), kind=kLoop, calls=%fused_computation.2 | loop fusion | flops 262144 | bytes 1053696 | tf_op jit(solution)/shard_map/mul | solution.py:24
  4.2 0.0 copy-start
  4.2 1.6 %copy-done = bf16[1024,1024]{1,0:T(8,128)(2,1)S(1)} copy-done((bf16[1024,1024]{1,0:T(8,128)(2,1)S(1)}, bf16[1024,1024]{1,0:T(8,128)(2,1)}, u32[]{:S(2)}) %copy-start) | copy-done | bytes 2097176
  5.8 0.0 copy-start.3
  5.8 1.2 %copy-done.3 = bf16[1024,512]{1,0:T(8,128)(2,1)S(1)} copy-done((bf16[1024,512]{1,0:T(8,128)(2,1)S(1)}, bf16[1024,512]{1,0:T(8,128)(2,1)}, u32[]{:S(2)}) %copy-start.3) | copy-done | bytes 1048600
  7.0 0.0 copy-start.4
  7.0 1.0 copy-done.4
  8.0 0.0 copy-start.5
  8.0 1.0 copy-done.5
  9.1 4.6 %proj.1 = (bf16[1024,1024]{1,0:T(8,128)(2,1)S(1)}, bf16[2,4,1024,128]{3,2,1,0:T(8,128)(2,1)S(1)}, bf16[1024,256]{1,0:T(8,128)(2,1)S(1)}, bf16[1024,256]{1,0:T(8,128)(2,1)S(1)}) custom-call(bf16[1024,1024]{1,0:T(8,128)(2,1)S(1)} %copy-done, f32[1024,128]{1,0:T(8,128)S(1)} %get-tuple-element.12.cos_ref, f32[1024,128]{1,0:T(8,128)S(1)} %get-tuple-element.11.sin_ref, ...), custom_call_target="tpu_custom_call" | custom-call | tf_op jit(solution)/shard_map/proj/pallas_call | solution.py:61
  13.6 0.0 copy-start.1
  13.7 1.3 %copy-done.1 = bf16[1024,1024]{1,0:T(8,128)(2,1)} copy-done((bf16[1024,1024]{1,0:T(8,128)(2,1)}, bf16[1024,1024]{1,0:T(8,128)(2,1)S(1)}, u32[]{:S(2)}) %copy-start.1) | copy-done | bytes 2097176
  15.0 0.0 copy-start.2
  15.0 1.3 %copy-done.2 = bf16[2,4,1024,128]{3,2,1,0:T(8,128)(2,1)} copy-done((bf16[2,4,1024,128]{3,2,1,0:T(8,128)(2,1)}, bf16[2,4,1024,128]{3,2,1,0:T(8,128)(2,1)S(1)}, u32[]{:S(2)}) %copy-start.2) | copy-done | bytes 2097176
  16.3 99.4 %layer.1 = bf16[1024,1024]{1,0:T(8,128)(2,1)} custom-call(bf16[1024,1024]{1,0:T(8,128)(2,1)} %copy-done.1, bf16[2,4,1024,128]{3,2,1,0:T(8,128)(2,1)} %copy-done.2, bf16[1024,1024]{1,0:T(8,128)(2,1)} %hid_hbm.1, bf16[1024,768]{1,0:T(8,128)(2,1)} %wg_hbm.1, bf16[1024,768]{1,0:T(8,128)(2,1)} %wu_hbm.1, bf16[768,1024]{1,0:T(8,128)(2,1)} %wd_hbm.1, ...), custom_call_target="tpu_custom_call" | custom-call | tf_op jit(solution)/shard_map/layer/pallas_call | solution.py:467
  115.8 0.9 reshape.37
  116.7 0.9 reshape.38
  117.6 3.1 %copy.14 = bf16[1024,1024]{1,0:T(8,128)(2,1)} copy(bf16[1024,1024]{1,0:T(8,128)(2,1)} %layer.1) | data formatting | bytes 4194304
  (2 shorter events, 0.0 us)
Async XLA Ops:
  4.2 1.6 %copy-start = (bf16[1024,1024]{1,0:T(8,128)(2,1)S(1)}, bf16[1024,1024]{1,0:T(8,128)(2,1)}, u32[]{:S(2)}) copy-start(bf16[1024,1024]{1,0:T(8,128)(2,1)} %hid_hbm.1) | copy-start | bytes 6291460
  5.8 1.2 %copy-start.3 = (bf16[1024,512]{1,0:T(8,128)(2,1)S(1)}, bf16[1024,512]{1,0:T(8,128)(2,1)}, u32[]{:S(2)}) copy-start(bf16[1024,512]{1,0:T(8,128)(2,1)} %wq_ref.1) | copy-start | bytes 3145732
  7.0 1.0 copy-start.4
  8.0 1.0 copy-start.5
  13.6 1.3 %copy-start.1 = (bf16[1024,1024]{1,0:T(8,128)(2,1)}, bf16[1024,1024]{1,0:T(8,128)(2,1)S(1)}, u32[]{:S(2)}) copy-start(bf16[1024,1024]{1,0:T(8,128)(2,1)S(1)} %get-tuple-element.7.h_hbm) | copy-start | bytes 6291460
  15.0 1.3 %copy-start.2 = (bf16[2,4,1024,128]{3,2,1,0:T(8,128)(2,1)}, bf16[2,4,1024,128]{3,2,1,0:T(8,128)(2,1)S(1)}, u32[]{:S(2)}) copy-start(bf16[2,4,1024,128]{3,2,1,0:T(8,128)(2,1)S(1)} %get-tuple-element.8.kvx_hbm) | copy-start | bytes 6291460

commit v2 on v1

v2 whole, which is shorter than its diff:
```python
import jax
import jax.numpy as jnp
import numpy as np
from jax import lax
from jax.experimental import pallas as pl
from jax.experimental.pallas import tpu as pltpu
from jax.sharding import PartitionSpec as P

HEAD_DIM = 128
ROPE_BASE = 4000000
LN_EPS = 1e-5
EXP2_SCALE = (HEAD_DIM ** -0.5) * 1.4426950408889634
MESH = pl.DeviceIdType.MESH
BF16 = jnp.bfloat16
F32 = jnp.float32


def sin_cos(angle):
    k = jnp.floor(angle * 0.6366197723675814 + 0.5)
    r = ((angle - k * 1.5703125) - k * 4.837512969970703125e-4) - k * 7.54978995489188216e-8
    z = r * r
    sn = r + r * z * (-1.6666654611e-1 + z * (8.3321608736e-3 - 1.9515295891e-4 * z))
    cs = 1.0 - 0.5 * z + z * z * (4.166664568298827e-2 + z * (-1.388731625493765e-3 + z * 2.443315711809948e-5))
    quad = k.astype(jnp.int32)
    odd = (quad & 1) == 1
    sin = jnp.where(odd, cs, sn)
    cos = jnp.where(odd, sn, cs)
    sin = jnp.where((quad & 2) == 2, -sin, sin)
    cos = jnp.where(((quad + 1) & 2) == 2, -cos, cos)
    return sin, cos


def layer_kernel(hid_hbm, pos_hbm, gain_hbm, freq_hbm, wq_hbm, wk_hbm, wv_hbm, wg_hbm, wu_hbm, wd_hbm, wo_hbm,
                 out_hbm, kc_hbm, vc_hbm,
                 kvbuf, qbuf, kvs, qs, acc, mbuf, lbuf, hid, h, pos, gain, freq, cost, sint,
                 wq, wk, wv, wg, wu, wd, wo, part, kc, vc,
                 osend, orecv, pbuf, rs1, sum2, rs2, xbuf,
                 load_sem, kvs_sem, kvr_sem, dds_sem, ddr_sem, ys_sem, yr_sem, out_sem):
    cp = lax.axis_index('cp')
    y = lax.axis_index('tp')
    x = cp // 2
    c = cp % 2
    partner = 2 * x + 1 - c
    right = ((x + 1) % 4) * 2 + c
    left = ((x + 3) % 4) * 2 + c
    y1 = y + 1 - 2 * (y % 2)
    y2 = 3 - y
    rows = hid_hbm.shape[0]
    sub = 256
    blocks = rows // sub
    quarter = sub // 4

    barrier = pltpu.get_barrier_semaphore()
    for dev in ({'cp': partner}, {'cp': right}, {'cp': left}, {'tp': y1}, {'tp': y2}):
        pl.semaphore_signal(barrier, inc=1, device_id=dev, device_id_type=MESH)

    pairs = ((hid_hbm, hid), (pos_hbm, pos), (gain_hbm, gain), (freq_hbm, freq), (wk_hbm, wk), (wv_hbm, wv), (wq_hbm, wq),
             (wg_hbm, wg), (wu_hbm, wu), (wd_hbm, wd), (wo_hbm, wo))
    loads = [pltpu.make_async_copy(src, dst, load_sem.at[i]) for i, (src, dst) in enumerate(pairs)]
    for i in (1, 3, 0, 2, 4, 5, 6):
        loads[i].start()

    def remote(src, dst, ss, rsem, dev):
        return pltpu.make_async_remote_copy(src_ref=src, dst_ref=dst, send_sem=ss, recv_sem=rsem,
                                            device_id=dev, device_id_type=MESH)

    def dd_kv(ch):
        return remote(kvs, kvbuf.at[ch], dds_sem.at[0], ddr_sem.at[0], {'cp': partner})

    def dd_q(half):
        return remote(qs, qbuf.at[half], dds_sem.at[1], ddr_sem.at[1], {'cp': partner})

    def kv_copy(ch, slot, dev):
        return remote(kvbuf.at[ch], kvbuf.at[ch], kvs_sem.at[slot], kvr_sem.at[ch], {'cp': dev})

    own_ch = 2 * x + c
    oth_ch = 2 * x + 1 - c

    loads[1].wait()
    loads[3].wait()
    lane = lax.broadcasted_iota(jnp.int32, (HEAD_DIM, HEAD_DIM), 1)
    for i in range(rows // HEAD_DIM):
        at = pl.ds(i * HEAD_DIM, HEAD_DIM)
        p = jnp.broadcast_to(pos[i:i + 1, :].astype(F32), (HEAD_DIM, HEAD_DIM)).T
        sn, cs = sin_cos(p * freq[...])
        cost[at, :] = cs
        sint[at, :] = jnp.where(lane % 2 == 0, -sn, sn)
    for i in (7, 8, 9, 10):
        loads[i].start()
    for i in (0, 2, 4, 5):
        loads[i].wait()

    even = lax.broadcasted_iota(jnp.int32, (sub, HEAD_DIM), 1) % 2 == 0
    gain_f = gain[...].astype(F32)
    gain_row = jnp.concatenate([gain_f[i:i + 1, :] for i in range(gain.shape[0])], axis=1)

    def rope(col, rs):
        u = col.astype(BF16).astype(F32)
        swapped = jnp.where(even, pltpu.roll(u, HEAD_DIM - 1, 1), pltpu.roll(u, 1, 1))
        return (u * cost[rs, :] + swapped * sint[rs, :]).astype(BF16)

    def project_kv(i, carry):
        rs = pl.ds(pl.multiple_of(i * sub, sub), sub)
        xx = hid[rs, :].astype(F32)
        cent = xx - jnp.mean(xx, axis=-1, keepdims=True)
        var = jnp.mean(cent * cent, axis=-1, keepdims=True)
        hh = (cent * lax.rsqrt(var + LN_EPS) * gain_row).astype(BF16)
        h[rs, :] = hh
        k = jnp.dot(hh, wk[...], preferred_element_type=F32)
        v = jnp.dot(hh, wv[...], preferred_element_type=F32).astype(BF16)
        vc[rs, :] = v
        for g in range(2):
            kc[rs, g * HEAD_DIM:(g + 1) * HEAD_DIM] = rope(k[:, g * HEAD_DIM:(g + 1) * HEAD_DIM], rs)

        def place(own, other):
            kvbuf[own_ch, 0, rs, :] = kc[rs, own * HEAD_DIM:(own + 1) * HEAD_DIM]
            kvbuf[own_ch, 1, rs, :] = vc[rs, own * HEAD_DIM:(own + 1) * HEAD_DIM]
            kvs[0, rs, :] = kc[rs, other * HEAD_DIM:(other + 1) * HEAD_DIM]
            kvs[1, rs, :] = vc[rs, other * HEAD_DIM:(other + 1) * HEAD_DIM]

        @pl.when(c == 0)
        def _():
            place(0, 1)

        @pl.when(c == 1)
        def _():
            place(1, 0)
        return carry

    with jax.named_scope('kvproj'):
        lax.fori_loop(0, rows // sub, project_kv, 0)
    pl.semaphore_wait(barrier, 5)
    dd_kv(own_ch).start()

    @pl.when(x < 3)
    def _():
        kv_copy(own_ch, 0, right).start()

    @pl.when(x == 0)
    def _():
        kv_copy(own_ch, 1, left).start()

    @pl.when(x == 1)
    def _():
        kv_copy(own_ch, 1, left).start()

    caches = (pltpu.make_async_copy(kc, kc_hbm, load_sem.at[11]), pltpu.make_async_copy(vc, vc_hbm, load_sem.at[12]))
    for cpy in caches:
        cpy.start()
    loads[6].wait()

    def project_q(i, carry):
        rs = pl.ds(pl.multiple_of(i * sub, sub), sub)
        q = jnp.dot(h[rs, :], wq[...], preferred_element_type=F32)
        for g in range(2):
            for j in range(2):
                lo = (2 * g + j) * HEAD_DIM
                qr = rope(q[:, lo:lo + HEAD_DIM], rs)

                @pl.when(c == g)
                def _():
                    qbuf[c, j, rs, :] = qr

                @pl.when(c != g)
                def _():
                    qs[j, rs, :] = qr
        return carry

    with jax.named_scope('qproj'):
        lax.fori_loop(0, rows // sub, project_q, 0)
    dd_q(c).start()
    dd_kv(oth_ch).wait_recv()

    @pl.when(x < 3)
    def _():
        kv_copy(oth_ch, 2, right).start()

    @pl.when(x == 0)
    def _():
        kv_copy(oth_ch, 3, left).start()

    loads[7].wait()
    loads[8].wait()
    loads[9].wait()

    def mlp(i, carry):
        rs = pl.ds(pl.multiple_of(i * sub, sub), sub)
        hh = h[rs, :]
        gate = jnp.dot(hh, wg[...], preferred_element_type=F32).astype(BF16).astype(F32)
        up = jnp.dot(hh, wu[...], preferred_element_type=F32).astype(BF16).astype(F32)
        a = (gate * (1.0 / (1.0 + jnp.exp(-gate))) * up).astype(BF16)
        part[rs, :] = jnp.dot(a, wd[...], preferred_element_type=F32)
        return carry

    with jax.named_scope('mlp'):
        lax.fori_loop(0, rows // sub, mlp, 0)

    dd_q(1 - c).wait_recv()

    def lane_sum(p):
        s = p[:, :HEAD_DIM]
        for j in range(1, p.shape[1] // HEAD_DIM):
            s = s + p[:, j * HEAD_DIM:(j + 1) * HEAD_DIM]
        return s

    def qk(qv, kv):
        return lax.dot_general(qv, kv, (((1,), (1,)), ((), ())), preferred_element_type=F32)

    k0, k1, v0, v1 = (kvbuf.at[2 * x, 0], kvbuf.at[2 * x + 1, 0], kvbuf.at[2 * x, 1], kvbuf.at[2 * x + 1, 1])
    tri = (lax.broadcasted_iota(jnp.int32, (sub, sub), 1) <= lax.broadcasted_iota(jnp.int32, (sub, sub), 0))
    groups = rows // sub

    def diag_scores(r, g):
        half, off = r // groups, (r % groups) * sub
        qv = qbuf[half, g, pl.ds(off, sub), :]
        pieces = []
        if half == 1:
            pieces.append(qk(qv, k0[...]))
        kk = k0 if half == 0 else k1
        if off:
            pieces.append(qk(qv, kk[pl.ds(0, off), :]))
        pieces.append(jnp.where(tri, qk(qv, kk[pl.ds(off, sub), :]), -jnp.inf))
        return pieces[0] if len(pieces) == 1 else jnp.concatenate(pieces, axis=1)

    def diag_soft(r, g, s):
        half, off = r // groups, (r % groups) * sub
        rs = pl.ds(off, sub)
        mx = jnp.max(s, axis=1, keepdims=True)
        p = jnp.exp2((s - mx) * EXP2_SCALE)
        pb = p.astype(BF16)
        if half == 0:
            o = jnp.dot(pb, v0[pl.ds(0, off + sub), :], preferred_element_type=F32)
        else:
            o = jnp.dot(pb[:, :rows], v0[...], preferred_element_type=F32)
            o = o + jnp.dot(pb[:, rows:], v1[pl.ds(0, off + sub), :], preferred_element_type=F32)
        mbuf[g, half, rs, :] = jnp.broadcast_to(mx, (sub, HEAD_DIM))
        lbuf[g, half, rs, :] = lane_sum(p)
        acc[g, half, rs, :] = o

    items = [(r, g) for r in range(2 * groups) for g in range(2)]
    own_block = jax.named_scope('diag')
    own_block.__enter__()
    s_now = diag_scores(*items[0])
    for i, it in enumerate(items):
        s_next = diag_scores(*items[i + 1]) if i + 1 < len(items) else None
        diag_soft(*it, s_now)
        s_now = s_next

    own_block.__exit__(None, None, None)
    loads[10].wait()

    @pl.when(x == 0)
    def _():
        kv_copy(2 + c, 0, right).wait_recv()
        kv_copy(2 + c, 4, left).start()

    def attend(chunks, its):
        def scores(it):
            g, half, rs = it
            qv = qbuf[half, g, rs, :]
            pieces = [qk(qv, kvbuf[ch, 0]) for ch in chunks]
            return pieces[0] if len(pieces) == 1 else jnp.concatenate(pieces, axis=1)

        s = scores(its[0])
        for i, it in enumerate(its):
            s_n = scores(its[i + 1]) if i + 1 < len(its) else None
            g, half, rs = it
            m_old = mbuf[g, half, rs, :]
            m_new = jnp.maximum(m_old, jnp.max(s, axis=1, keepdims=True))
            alpha = jnp.exp2((m_old - m_new) * EXP2_SCALE)
            p = jnp.exp2((s - m_new[:, :1]) * EXP2_SCALE)
            lbuf[g, half, rs, :] = lbuf[g, half, rs, :] * alpha + lane_sum(p)
            pb = p.astype(BF16)
            o = acc[g, half, rs, :] * alpha
            for i_ch, ch in enumerate(chunks):
                o = o + jnp.dot(pb[:, i_ch * rows:(i_ch + 1) * rows], kvbuf[ch, 1], preferred_element_type=F32)
            acc[g, half, rs, :] = o
            mbuf[g, half, rs, :] = m_new
            s = s_n

    def block_rows(b):
        return pl.ds(pl.multiple_of(b * sub, sub), sub)

    def attend_pair(ch, pair):
        attend((ch,), [(g, half, block_rows(2 * pair + j)) for half in range(2) for j in range(2) for g in range(2)])

    def attend_last(ch_a, ch_b, b):
        attend((ch_a, ch_b), [(g, half, block_rows(b)) for half in range(2) for g in range(2)])

    first = (y1, y2)
    second = (y2, y1)

    def y_copy(src, dst, b, i, dev):
        return remote(src, dst, ys_sem.at[b, i], yr_sem.at[b, i], {'tp': dev})

    def rs1_copy(b, hf, slot):
        dev = first[hf]
        far = (3 - dev) if hf == 0 else (dev + 1 - 2 * (dev % 2))
        tile = dev if slot == 0 else far
        return y_copy(pbuf.at[b, tile, hf], rs1.at[b, hf, slot], b, 2 * hf + slot, dev)

    def rs2_copy(b, hf):
        return y_copy(sum2.at[b, hf], rs2.at[b, hf], b, 4 + hf, second[hf])

    def ag1_copy(b, hf):
        return y_copy(xbuf.at[b, y, hf], xbuf.at[b, y, hf], b, 6 + hf, second[hf])

    def ag1_wait(b, hf):
        t = second[hf]
        y_copy(xbuf.at[b, t, hf], xbuf.at[b, t, hf], b, 6 + hf, t).wait_recv()

    def ag2_copy(b, hf, slot):
        t = y if slot == 0 else second[hf]
        return y_copy(xbuf.at[b, t, hf], xbuf.at[b, t, hf], b, 8 + 2 * hf + slot, first[hf])

    def ag2_wait(b, hf, slot):
        dev = first[hf]
        far = (3 - dev) if hf == 0 else (dev + 1 - 2 * (dev % 2))
        t = dev if slot == 0 else far
        y_copy(xbuf.at[b, t, hf], xbuf.at[b, t, hf], b, 8 + 2 * hf + slot, dev).wait_recv()

    def o_copy(b):
        return remote(osend.at[b], orecv.at[b], dds_sem.at[2 + b], ddr_sem.at[2 + b], {'cp': partner})

    cols = (0, 512)

    def finish(b):
        rs = block_rows(b)

        def norm(half):
            out = []
            for g in range(2):
                den = jnp.sum(lbuf[g, half, rs, :], axis=1, keepdims=True)
                out.append((acc[g, half, rs, :] / den).astype(BF16))
            return jnp.concatenate(out, axis=1)

        def wo_rows(group):
            return wo[pl.ds(pl.multiple_of(group * 2 * HEAD_DIM, 2 * HEAD_DIM), 2 * HEAD_DIM), :]

        osend[b] = norm(1 - c)
        o_copy(b).start()
        part[rs, :] = part[rs, :] + jnp.dot(norm(c), wo_rows(c), preferred_element_type=F32)
        o_copy(b).wait_recv()
        tot = (part[rs, :] + jnp.dot(orecv[b], wo_rows(1 - c), preferred_element_type=F32)).astype(BF16)
        for j in range(4):
            for hf in range(2):
                pbuf[b, j, hf] = tot[j * quarter:(j + 1) * quarter, cols[hf]:cols[hf] + 512]
        for slot in (1, 0):
            for hf in range(2):
                rs1_copy(b, hf, slot).start()

    def step1(b):
        for hf in range(2):
            rs1_copy(b, hf, 1).wait_recv()
            other = second[hf]
            sum2[b, hf] = (pbuf[b, other, hf].astype(F32) + rs1[b, hf, 1].astype(F32)).astype(BF16)
            rs2_copy(b, hf).start()

    def step2(b):
        own_rows = pl.ds(pl.multiple_of(b * sub + y * quarter, quarter), quarter)
        for hf in range(2):
            rs1_copy(b, hf, 0).wait_recv()
            rs2_copy(b, hf).wait_recv()
            tot = pbuf[b, y, hf].astype(F32) + rs1[b, hf, 0].astype(F32) + rs2[b, hf].astype(F32)
            tot = tot + hid[own_rows, cols[hf]:cols[hf] + 512].astype(F32)
            xbuf[b, y, hf] = tot.astype(BF16)
            ag1_copy(b, hf).start()
        for hf in range(2):
            ag2_copy(b, hf, 0).start()

    def step3(b):
        for hf in range(2):
            ag1_wait(b, hf)
            ag2_copy(b, hf, 1).start()

    def out_copy(b, t, hf):
        return pltpu.make_async_copy(
            xbuf.at[b, t, hf],
            out_hbm.at[pl.ds(b * sub + t * quarter, quarter), pl.ds(cols[hf], 512)],
            out_sem.at[b, t, hf])

    def step4(b):
        for hf in range(2):
            for slot in range(2):
                ag2_wait(b, hf, slot)
        for t in range(4):
            for hf in range(2):
                out_copy(b, t, hf).start()

    n = 2 * x

    def chunk_of(s):
        first_half = s // 2
        par = s % 2
        near = 2 * (x - 1 - first_half) + (c + par - 2 * c * par)
        mix_half = c + first_half - 2 * c * first_half
        mixed = 4 - 4 * par + mix_half
        late = 2 + (c + par - 2 * c * par)
        three = jnp.where(s < 4, mixed, late)
        return jnp.where(x == 3, three, near)

    three = x == 3
    lead = 4 * (x // 2) + 2 * (x // 3)
    ticks = lead + 8 + 2 * (x // 3)

    def pick(tau, near, far):
        b = jnp.int32(-1)
        for i in range(4):
            b = jnp.where(tau == jnp.where(three, far[i], near[i]), i, b)
        return jnp.maximum(b, 0), b >= 0

    def loop(t, carry):
        tau = t - lead
        gap = jnp.logical_and(three, jnp.logical_or(tau == 1, tau == 3))
        s3 = jnp.where(t == 0, 0, jnp.where(t == 1, 1, jnp.where(t == 2, 0, jnp.where(t == 3, 2, jnp.where(
            t == 4, 3, jnp.where(t == 5, 1, jnp.where(tau == 1, 2, 3)))))))
        pair3 = jnp.where(jnp.logical_or(t == 2, t >= 5), 1, 0)
        s = jnp.where(three, s3, t // 2)
        pair = jnp.where(three, pair3, t % 2)

        @pl.when(jnp.logical_and(x == 2, jnp.logical_and(tau < 0, t % 2 == 0)))
        def _():
            kv_copy(chunk_of(s), 0, right).wait_recv()

            @pl.when(t == 2)
            def _():
                kv_copy(chunk_of(1), 1, right).start()

        @pl.when(jnp.logical_and(three, jnp.logical_or(t == 0, t == 3)))
        def _():
            ch_b = chunk_of(s + 1)
            kv_copy(ch_b, 0, right).wait_recv()

            @pl.when(t == 0)
            def _():
                kv_copy(ch_b, 0, left).start()

            kv_copy(chunk_of(s), 0, right).wait_recv()

        @pl.when(jnp.logical_and(x > 0, tau == 0))
        def _():
            kv_copy(chunk_of(n - 2), 0, right).wait_recv()
            kv_copy(chunk_of(n - 1), 0, right).wait_recv()

            @pl.when(x == 1)
            def _():
                kv_copy(chunk_of(1), 3, right).start()

        @pl.when(jnp.logical_or(tau < 0, gap))
        def _():
            with jax.named_scope('att'):
                attend_pair(chunk_of(s), pair)

        b0, ok0 = pick(tau, (0, 1, 2, 3), (0, 2, 4, 5))

        @pl.when(jnp.logical_and(ok0, x > 0))
        def _():
            with jax.named_scope('last'):
                attend_last(chunk_of(n - 2), chunk_of(n - 1), b0)

        for fn, nm, near, far in ((step1, 's1', (2, 3, 4, 5), (2, 4, 6, 7)),
                                  (step2, 's2', (3, 4, 5, 6), (3, 5, 7, 8)),
                                  (step3, 's3', (4, 5, 6, 7), (4, 6, 8, 9))):
            bk, okk = pick(tau, near, far)

            @pl.when(okk)
            def _():
                with jax.named_scope(nm):
                    fn(bk)

        @pl.when(ok0)
        def _():
            with jax.named_scope('finish'):
                finish(b0)
        return carry

    lax.fori_loop(0, ticks, loop, 0)

    def last_step(b, carry):
        with jax.named_scope('s4'):
            step4(b)
        return carry

    lax.fori_loop(0, blocks, last_step, 0)

    dd_kv(own_ch).wait_send()
    dd_q(c).wait_send()
    for cpy in caches:
        cpy.wait()

    @pl.when(x < 3)
    def _():
        kv_copy(own_ch, 0, right).wait_send()
        kv_copy(own_ch, 1, right).wait_send()
        kv_copy(oth_ch, 2, right).wait_send()

    @pl.when(x == 0)
    def _():
        kv_copy(oth_ch, 3, left).wait_send()
        kv_copy(oth_ch, 4, left).wait_send()

    @pl.when(x == 1)
    def _():
        kv_copy(own_ch, 3, left).wait_send()

    @pl.when(x == 3)
    def _():
        kv_copy(own_ch, 0, left).wait_send()

    for b in range(blocks):
        o_copy(b).wait_send()
        for hf in range(2):
            rs2_copy(b, hf).wait_send()
            ag1_copy(b, hf).wait_send()
            for slot in range(2):
                rs1_copy(b, hf, slot).wait_send()
                ag2_copy(b, hf, slot).wait_send()
        for t in range(4):
            for hf in range(2):
                out_copy(b, t, hf).wait()


def layer(hidden, positions, gain, w_q, w_k, w_v, w_gate, w_up, w_down, w_o):
    rows, width = hidden.shape
    ff = w_gate.shape[1]
    hr = 256
    nb = rows // hr
    qr = hr // 4
    hw = width // 2
    freq = 1.0 / (ROPE_BASE ** (np.repeat(np.arange(0, HEAD_DIM, 2), 2) / HEAD_DIM))
    freq = jnp.asarray(freq[None, :], F32)
    anyspec = pl.BlockSpec(memory_space=pl.ANY)
    vm = pltpu.VMEM
    dma = pltpu.SemaphoreType.DMA
    return pl.pallas_call(
        layer_kernel,
        in_specs=[anyspec] * 11,
        out_specs=[anyspec] * 3,
        out_shape=[jax.ShapeDtypeStruct((rows, width), BF16),
                   jax.ShapeDtypeStruct((rows, w_k.shape[1]), BF16),
                   jax.ShapeDtypeStruct((rows, w_v.shape[1]), BF16)],
        scratch_shapes=[
            vm((8, 2, rows, HEAD_DIM), BF16),
            vm((2, 2, rows, HEAD_DIM), BF16),
            vm((2, rows, HEAD_DIM), BF16),
            vm((2, rows, HEAD_DIM), BF16),
            vm((2, 2, rows, HEAD_DIM), F32),
            vm((2, 2, rows, HEAD_DIM), F32),
            vm((2, 2, rows, HEAD_DIM), F32),
            vm((rows, width), BF16),
            vm((rows, width), BF16),
            vm((rows // HEAD_DIM, HEAD_DIM), jnp.int32),
            vm((width // HEAD_DIM, HEAD_DIM), BF16),
            vm((1, HEAD_DIM), F32),
            vm((rows, HEAD_DIM), F32),
            vm((rows, HEAD_DIM), F32),
            vm(w_q.shape, BF16), vm(w_k.shape, BF16), vm(w_v.shape, BF16),
            vm((width, ff), BF16), vm((width, ff), BF16), vm((ff, width), BF16),
            vm(w_o.shape, BF16),
            vm((rows, width), F32),
            vm((rows, w_k.shape[1]), BF16),
            vm((rows, w_v.shape[1]), BF16),
            vm((nb, hr, 2 * HEAD_DIM), BF16),
            vm((nb, hr, 2 * HEAD_DIM), BF16),
            vm((nb, 4, 2, qr, hw), BF16),
            vm((nb, 2, 2, qr, hw), BF16),
            vm((nb, 2, qr, hw), BF16),
            vm((nb, 2, qr, hw), BF16),
            vm((nb, 4, 2, qr, hw), BF16),
            dma((13,)), dma((5,)), dma((8,)), dma((2 + nb,)), dma((2 + nb,)), dma((nb, 12)), dma((nb, 12)), dma((nb, 4, 2)),
        ],
        compiler_params=pltpu.CompilerParams(collective_id=0, has_side_effects=True, vmem_limit_bytes=62 << 20),
        name='layer',
    )(hidden, positions.reshape(rows // HEAD_DIM, HEAD_DIM), gain.reshape(width // HEAD_DIM, HEAD_DIM), freq,
      w_q, w_k, w_v, w_gate, w_up, w_down, w_o)


def solution(mesh):
    def local_layer(hidden, positions, ln_gain, w_q, w_k, w_v, w_o, w_gate, w_up, w_down):
        rows = hidden.shape[0]
        kv_local = w_k.shape[1] // HEAD_DIM
        out, kc, vc = layer(hidden, positions, ln_gain, w_q, w_k, w_v, w_gate, w_up, w_down, w_o)
        return out, kc.reshape(rows, kv_local, HEAD_DIM), vc.reshape(rows, kv_local, HEAD_DIM)

    row_spec = P(('dp', 'cp'), None)
    col_spec = P(None, 'tp')
    cache_spec = P(('dp', 'cp'), 'tp', None)
    in_specs = (row_spec, P(('dp', 'cp')), P(None), col_spec, col_spec, col_spec, P('tp', None), col_spec, col_spec, P('tp', None))
    return jax.shard_map(local_layer, mesh=mesh, in_specs=in_specs, out_specs=(row_spec, cache_spec, cache_spec), check_vma=False)
```

time: 121 us -> 97.6 us (0.81)
  Pallas kernels: 104 us -> 91.4 us
  local copies, waits for them, and re-layouts: 13.4 us -> 5.39 us
  other arithmetic: 2.61 us -> 0 us
    pallas_call x2 -> x1, Pallas kernels: 104 us -> 91.4 us  [layer(): pl.pallas_call(layer_kernel, in_specs=[anyspec] * 11, out_specs=[anyspec]...]
    unnamed x13 -> x3, local copies, waits for them, and re-layouts: 10.6 us -> 1.32 us
    mul x1 -> x0, other arithmetic: 1.9 us -> none  [rope_tables(): return (jnp.cos(angles), jnp.sin(angles) * sign[None, :])]
where the time goes in v2:
time: 97.6 us; the launch traced here: 97.4 us
  Pallas kernels  91.4 us (94%)
  local copies, waits for them, and re-layouts  5.39 us (6%)
    pallas_call x1, Pallas kernels, layer(): pl.pallas_call(layer_kernel, in_specs=[anyspec] * 11, out_specs=[anyspec]...  91.4 us
    reshape x1, local copies, waits for them, and re-layouts, local_layer(): kc.reshape(rows, kv_local, HEAD_DIM)  2.11 us
    reshape x1, local copies, waits for them, and re-layouts, local_layer(): vc.reshape(rows, kv_local, HEAD_DIM)  1.96 us

profile of v2, /device:TPU:102, one launch (start us, length us, event | category | flops | bytes accessed | tf_op | source)
XLA Modules:
  0.0 97.4 jit_solution(10512921682552288799)
XLA Ops:
  0.6 91.4 %layer.1 = (bf16[1024,1024]{1,0:T(8,128)(2,1)}, bf16[1024,256]{1,0:T(8,128)(2,1)}, bf16[1024,256]{1,0:T(8,128)(2,1)}) custom-call(bf16[1024,1024]{1,0:T(8,128)(2,1)} %hid_hbm.1, s32[8,128]{1,0:T(8,128)} %bitcast.2, bf16[8,128]{1,0:T(8,128)(2,1)} %bitcast.3, f32[1,128]{1,0:T(1,128)} %constant.2.clone.freq_hbm, bf16[1024,512]{1,0:T(8,128)(2,1)} %wq_hbm.1, ...), custom_call_target="tpu_custom_call" | custom-call | tf_op jit(solution)/shard_map/layer/pallas_call | solution.py:535
  92.0 0.0 copy-start
  92.0 2.1 %reshape.20 = bf16[1024,2,128]{2,1,0:T(2,128)(2,1)} reshape(bf16[1024,256]{1,0:T(8,128)(2,1)} %get-tuple-element.7) | data formatting | bytes 1048576 | tf_op jit(solution)/shard_map/reshape | solution.py:583
  94.1 2.0 %reshape.21 = bf16[1024,2,128]{2,1,0:T(2,128)(2,1)} reshape(bf16[1024,256]{1,0:T(8,128)(2,1)} %get-tuple-element.8) | data formatting | bytes 1048576 | tf_op jit(solution)/shard_map/reshape | solution.py:583
  96.1 0.0 copy-done
  96.1 1.3 %copy.15 = bf16[1024,1024]{1,0:T(8,128)(2,1)} copy(bf16[1024,1024]{1,0:T(8,128)(2,1)S(1)} %copy-done) | data formatting | bytes 4194304
Async XLA Ops:
  92.0 4.1 %copy-start = (bf16[1024,1024]{1,0:T(8,128)(2,1)S(1)}, bf16[1024,1024]{1,0:T(8,128)(2,1)}, u32[]{:S(2)}) copy-start(bf16[1024,1024]{1,0:T(8,128)(2,1)} %get-tuple-element.12) | copy-start | bytes 6291460

commit v3 on v2

--- a/solution.py
+++ b/solution.py
@@ -33,9 +33,9 @@
 def layer_kernel(hid_hbm, pos_hbm, gain_hbm, freq_hbm, wq_hbm, wk_hbm, wv_hbm, wg_hbm, wu_hbm, wd_hbm, wo_hbm,
                  out_hbm, kc_hbm, vc_hbm,
                  kvbuf, qbuf, kvs, qs, acc, mbuf, lbuf, hid, h, pos, gain, freq, cost, sint,
-                 wq, wk, wv, wg, wu, wd, wo, part, kc, vc,
-                 osend, orecv, pbuf, rs1, sum2, rs2, xbuf,
-                 load_sem, kvs_sem, kvr_sem, dds_sem, ddr_sem, ys_sem, yr_sem, out_sem):
+                 wq, wk, wv, wg, wu, wd, wo, wide, kc, vc,
+                 mpart, mrs1, msum, mrs2, obuf, orecv, orelay, out,
+                 load_sem, hid_sem, kvs_sem, kvr_sem, dds_sem, ddr_sem, es_sem, er_sem, ys_sem, yr_sem, out_sem):
     cp = lax.axis_index('cp')
     y = lax.axis_index('tp')
     x = cp // 2
@@ -51,13 +51,25 @@
     quarter = sub // 4
 
     barrier = pltpu.get_barrier_semaphore()
-    for dev in ({'cp': partner}, {'cp': right}, {'cp': left}, {'tp': y1}, {'tp': y2}):
+    for dev in ({'cp': partner}, {'cp': right}, {'cp': left}, {'tp': y1}, {'tp': y2},
+                {'tp': y1, 'cp': partner}, {'tp': y2, 'cp': partner}):
         pl.semaphore_signal(barrier, inc=1, device_id=dev, device_id_type=MESH)
 
     pairs = ((hid_hbm, hid), (pos_hbm, pos), (gain_hbm, gain), (freq_hbm, freq), (wk_hbm, wk), (wv_hbm, wv), (wq_hbm, wq),
-             (wg_hbm, wg), (wu_hbm, wu), (wd_hbm, wd), (wo_hbm, wo))
+             (wg_hbm, wg), (wu_hbm, wu), (wd_hbm, wd), (wo_hbm, wo.at[y]))
     loads = [pltpu.make_async_copy(src, dst, load_sem.at[i]) for i, (src, dst) in enumerate(pairs)]
-    for i in (1, 3, 0, 2, 4, 5, 6):
+    def hid_tile(i):
+        rs = pl.ds(pl.multiple_of(i * sub, sub), sub)
+        return pltpu.make_async_copy(hid_hbm.at[rs], hid.at[rs], hid_sem.at[i])
+
+    loads[1].start()
+    loads[3].start()
+    hid_tile(0).start()
+    for i in (2, 4, 5):
+        loads[i].start()
+    for i in range(1, blocks):
+        hid_tile(i).start()
+    for i in (6, 10):
         loads[i].start()
 
     def remote(src, dst, ss, rsem, dev):
@@ -70,8 +82,59 @@
     def dd_q(half):
         return remote(qs, qbuf.at[half], dds_sem.at[1], ddr_sem.at[1], {'cp': partner})
 
-    def kv_copy(ch, slot, dev):
-        return remote(kvbuf.at[ch], kvbuf.at[ch], kvs_sem.at[slot], kvr_sem.at[ch], {'cp': dev})
+    class KvCopy:
+        def __init__(self, ch, slot, dev):
+            self.parts = []
+            for p in range(2):
+                ref = kvbuf.at[ch, :, pl.ds(p * (rows // 2), rows // 2)]
+                self.parts.append(remote(ref, ref, kvs_sem.at[slot, p], kvr_sem.at[ch, p], {'cp': dev}))
+
+        def start(self):
+            for part in self.parts:
+                part.start()
+
+        def wait_recv(self):
+            for part in self.parts:
+                part.wait_recv()
+
+        def wait_send(self):
+            for part in self.parts:
+                part.wait_send()
+
+    kv_copy = KvCopy
+
+    first = (y1, y2)
+    second = (y2, y1)
+    far = 3 - y1
+
+    def e_copy(src, dst, i, dev):
+        return remote(src, dst, es_sem.at[i], er_sem.at[i], dev)
+
+    w_half = 2 * HEAD_DIM
+
+    def wo_rows(shard, lo, size):
+        return wo.at[shard, pl.ds(pl.multiple_of(c * w_half + lo, HEAD_DIM), size)]
+
+    def wo_direct(i, shard):
+        ref = wo_rows(shard, 0, w_half)
+        return e_copy(ref, ref, i, {'tp': first[i]})
+
+    def wo_relay(hf, shard):
+        ref = wo_rows(shard, hf * HEAD_DIM, HEAD_DIM)
+        return e_copy(ref, ref, 2 + hf, {'tp': first[hf]})
+
+    def wo_partner(i):
+        ref = wo_rows((y1, y2, far)[i], 0, w_half)
+        return e_copy(ref, ref, 4 + i, {'cp': partner})
+
+    def mlp_rs1(hf, slot):
+        dev = first[hf]
+        beyond = (3 - dev) if hf == 0 else (dev + 1 - 2 * (dev % 2))
+        tile = dev if slot == 0 else beyond
+        return e_copy(mpart.at[tile, hf], mrs1.at[hf, slot], 7 + 2 * hf + slot, {'tp': dev})
+
+    def mlp_rs2(hf):
+        return e_copy(msum.at[hf], mrs2.at[hf], 11 + hf, {'tp': second[hf]})
 
     own_ch = 2 * x + c
     oth_ch = 2 * x + 1 - c
@@ -85,9 +148,9 @@
         sn, cs = sin_cos(p * freq[...])
         cost[at, :] = cs
         sint[at, :] = jnp.where(lane % 2 == 0, -sn, sn)
-    for i in (7, 8, 9, 10):
+    for i in (7, 8, 9):
         loads[i].start()
-    for i in (0, 2, 4, 5):
+    for i in (2, 4, 5):
         loads[i].wait()
 
     even = lax.broadcasted_iota(jnp.int32, (sub, HEAD_DIM), 1) % 2 == 0
@@ -101,6 +164,7 @@
 
     def project_kv(i, carry):
         rs = pl.ds(pl.multiple_of(i * sub, sub), sub)
+        hid_tile(i).wait()
         xx = hid[rs, :].astype(F32)
         cent = xx - jnp.mean(xx, axis=-1, keepdims=True)
         var = jnp.mean(cent * cent, axis=-1, keepdims=True)
@@ -108,15 +172,19 @@
         h[rs, :] = hh
         k = jnp.dot(hh, wk[...], preferred_element_type=F32)
         v = jnp.dot(hh, wv[...], preferred_element_type=F32).astype(BF16)
-        vc[rs, :] = v
-        for g in range(2):
-            kc[rs, g * HEAD_DIM:(g + 1) * HEAD_DIM] = rope(k[:, g * HEAD_DIM:(g + 1) * HEAD_DIM], rs)
+        kk = [rope(k[:, g * HEAD_DIM:(g + 1) * HEAD_DIM], rs) for g in range(2)]
+        vv = [v[:, g * HEAD_DIM:(g + 1) * HEAD_DIM] for g in range(2)]
+        pair_rows = pl.ds(pl.multiple_of(i * 2 * sub, 2 * sub), 2 * sub)
+        for slot, (vals, out) in enumerate(((kk, kc), (vv, vc))):
+            for g in range(2):
+                wide[slot, pl.ds(g, sub, 2), :] = vals[g].astype(F32)
+            out[pair_rows, :] = wide[slot].astype(BF16)
 
         def place(own, other):
-            kvbuf[own_ch, 0, rs, :] = kc[rs, own * HEAD_DIM:(own + 1) * HEAD_DIM]
-            kvbuf[own_ch, 1, rs, :] = vc[rs, own * HEAD_DIM:(own + 1) * HEAD_DIM]
-            kvs[0, rs, :] = kc[rs, other * HEAD_DIM:(other + 1) * HEAD_DIM]
-            kvs[1, rs, :] = vc[rs, other * HEAD_DIM:(other + 1) * HEAD_DIM]
+            kvbuf[own_ch, 0, rs, :] = kk[own]
+            kvbuf[own_ch, 1, rs, :] = vv[own]
+            kvs[0, rs, :] = kk[other]
+            kvs[1, rs, :] = vv[other]
 
         @pl.when(c == 0)
         def _():
@@ -127,22 +195,28 @@
             place(1, 0)
         return carry
 
+    def send_own(p):
+        @pl.when(x < 3)
+        def _():
+            kv_copy(own_ch, 0, right).parts[p].start()
+
+        @pl.when(x < 2)
+        def _():
+            kv_copy(own_ch, 1, left).parts[p].start()
+
     with jax.named_scope('kvproj'):
-        lax.fori_loop(0, rows // sub, project_kv, 0)
-    pl.semaphore_wait(barrier, 5)
+        lax.fori_loop(0, blocks // 2, project_kv, 0)
+    with jax.named_scope('bar'):
+        pl.semaphore_wait(barrier, 7)
+    send_own(0)
+    with jax.named_scope('kvproj'):
+        lax.fori_loop(blocks // 2, blocks, project_kv, 0)
+    send_own(1)
     dd_kv(own_ch).start()
 
-    @pl.when(x < 3)
-    def _():
-        kv_copy(own_ch, 0, right).start()
-
-    @pl.when(x == 0)
-    def _():
-        kv_copy(own_ch, 1, left).start()
-
-    @pl.when(x == 1)
-    def _():
-        kv_copy(own_ch, 1, left).start()
+    loads[10].wait()
+    for i in range(2):
+        wo_direct(i, y).start()
 
     caches = (pltpu.make_async_copy(kc, kc_hbm, load_sem.at[11]), pltpu.make_async_copy(vc, vc_hbm, load_sem.at[12]))
     for cpy in caches:
@@ -183,18 +257,26 @@
     loads[8].wait()
     loads[9].wait()
 
+    cols = (0, 512)
+
     def mlp(i, carry):
         rs = pl.ds(pl.multiple_of(i * sub, sub), sub)
         hh = h[rs, :]
         gate = jnp.dot(hh, wg[...], preferred_element_type=F32).astype(BF16).astype(F32)
         up = jnp.dot(hh, wu[...], preferred_element_type=F32).astype(BF16).astype(F32)
         a = (gate * (1.0 / (1.0 + jnp.exp(-gate))) * up).astype(BF16)
-        part[rs, :] = jnp.dot(a, wd[...], preferred_element_type=F32)
+        tot = jnp.dot(a, wd[...], preferred_element_type=F32).astype(BF16)
+        for j in range(4):
+            for hf in range(2):
+                mpart[j, hf, i] = tot[j * quarter:(j + 1) * quarter, cols[hf]:cols[hf] + 512]
         return carry
 
     with jax.named_scope('mlp'):
         lax.fori_loop(0, rows // sub, mlp, 0)
 
+    for slot in (1, 0):
+        for hf in range(2):
+            mlp_rs1(hf, slot).start()
     dd_q(1 - c).wait_recv()
 
     def lane_sum(p):
@@ -247,7 +329,9 @@
         s_now = s_next
 
     own_block.__exit__(None, None, None)
-    loads[10].wait()
+    for hf in range(2):
+        wo_direct(1 - hf, second[hf]).wait_recv()
+        wo_relay(hf, second[hf]).start()
 
     @pl.when(x == 0)
     def _():
@@ -281,111 +365,176 @@
     def block_rows(b):
         return pl.ds(pl.multiple_of(b * sub, sub), sub)
 
-    def attend_pair(ch, pair):
-        attend((ch,), [(g, half, block_rows(2 * pair + j)) for half in range(2) for j in range(2) for g in range(2)])
+    def attend_pair(ch_a, ch_b, pair):
+        attend((ch_a, ch_b), [(g, half, block_rows(2 * pair + j)) for half in range(2) for j in range(2) for g in range(2)])
 
     def attend_last(ch_a, ch_b, b):
         attend((ch_a, ch_b), [(g, half, block_rows(b)) for half in range(2) for g in range(2)])
 
-    first = (y1, y2)
-    second = (y2, y1)
-
     def y_copy(src, dst, b, i, dev):
-        return remote(src, dst, ys_sem.at[b, i], yr_sem.at[b, i], {'tp': dev})
-
-    def rs1_copy(b, hf, slot):
-        dev = first[hf]
-        far = (3 - dev) if hf == 0 else (dev + 1 - 2 * (dev % 2))
-        tile = dev if slot == 0 else far
-        return y_copy(pbuf.at[b, tile, hf], rs1.at[b, hf, slot], b, 2 * hf + slot, dev)
-
-    def rs2_copy(b, hf):
-        return y_copy(sum2.at[b, hf], rs2.at[b, hf], b, 4 + hf, second[hf])
+        return remote(src, dst, ys_sem.at[b, i], yr_sem.at[b, i], dev)
+
+    def o_direct(b, i, core):
+        return remote(obuf.at[b, first[i], core], orecv.at[b, y, c], ys_sem.at[b, 2 * i + core], yr_sem.at[b, 2 * i + c],
+                      {'tp': first[i], 'cp': 2 * x + core})
+
+    def o_direct_wait(b, i, core):
+        y_copy(obuf.at[b, y, c], orecv.at[b, first[i], core], b, 2 * i + core, {'tp': y1}).wait_recv()
+
+    def o_far(b, hf, core):
+        return remote(obuf.at[b, far, core, hf], orelay.at[b, hf, c], ys_sem.at[b, 4 + 2 * hf + core], yr_sem.at[b, 4 + 2 * hf + c],
+                      {'tp': first[hf], 'cp': 2 * x + core})
+
+    def o_far_wait(b, hf, core):
+        y_copy(obuf.at[b, far, core, hf], orelay.at[b, hf, core], b, 4 + 2 * hf + core, {'tp': y1}).wait_recv()
+
+    def o_relay(b, hf):
+        return y_copy(orelay.at[b, hf], orecv.at[b, first[hf], :, hf], b, 8 + hf, {'tp': second[hf]})
+
+    def o_relay_wait(b, hf):
+        y_copy(orelay.at[b, hf], orecv.at[b, far, :, hf], b, 8 + hf, {'tp': y1}).wait_recv()
+
+    def o_partner(b):
+        return y_copy(obuf.at[b, y, 1 - c], orecv.at[b, y, c], b, 10, {'cp': partner})
+
+    def o_partner_wait(b):
+        y_copy(obuf.at[b, y, c], orecv.at[b, y, 1 - c], b, 10, {'cp': partner}).wait_recv()
+
+    def xt(b, t, hf):
+        return out.at[pl.ds(pl.multiple_of(b * sub + t * quarter, quarter), quarter), pl.ds(cols[hf], 512)]
 
     def ag1_copy(b, hf):
-        return y_copy(xbuf.at[b, y, hf], xbuf.at[b, y, hf], b, 6 + hf, second[hf])
+        return y_copy(xt(b, y, hf), xt(b, y, hf), b, 11 + hf, {'tp': second[hf]})
 
     def ag1_wait(b, hf):
         t = second[hf]
-        y_copy(xbuf.at[b, t, hf], xbuf.at[b, t, hf], b, 6 + hf, t).wait_recv()
+        y_copy(xt(b, t, hf), xt(b, t, hf), b, 11 + hf, {'tp': t}).wait_recv()
 
     def ag2_copy(b, hf, slot):
         t = y if slot == 0 else second[hf]
-        return y_copy(xbuf.at[b, t, hf], xbuf.at[b, t, hf], b, 8 + 2 * hf + slot, first[hf])
+        return y_copy(xt(b, t, hf), xt(b, t, hf), b, 13 + 2 * hf + slot, {'tp': first[hf]})
 
     def ag2_wait(b, hf, slot):
         dev = first[hf]
-        far = (3 - dev) if hf == 0 else (dev + 1 - 2 * (dev % 2))
         t = dev if slot == 0 else far
-        y_copy(xbuf.at[b, t, hf], xbuf.at[b, t, hf], b, 8 + 2 * hf + slot, dev).wait_recv()
-
-    def o_copy(b):
-        return remote(osend.at[b], orecv.at[b], dds_sem.at[2 + b], ddr_sem.at[2 + b], {'cp': partner})
-
-    cols = (0, 512)
+        y_copy(xt(b, t, hf), xt(b, t, hf), b, 13 + 2 * hf + slot, {'tp': dev}).wait_recv()
 
     def finish(b):
         rs = block_rows(b)
-
-        def norm(half):
-            out = []
+        for half in range(2):
             for g in range(2):
                 den = jnp.sum(lbuf[g, half, rs, :], axis=1, keepdims=True)
-                out.append((acc[g, half, rs, :] / den).astype(BF16))
-            return jnp.concatenate(out, axis=1)
-
-        def wo_rows(group):
-            return wo[pl.ds(pl.multiple_of(group * 2 * HEAD_DIM, 2 * HEAD_DIM), 2 * HEAD_DIM), :]
-
-        osend[b] = norm(1 - c)
-        o_copy(b).start()
-        part[rs, :] = part[rs, :] + jnp.dot(norm(c), wo_rows(c), preferred_element_type=F32)
-        o_copy(b).wait_recv()
-        tot = (part[rs, :] + jnp.dot(orecv[b], wo_rows(1 - c), preferred_element_type=F32)).astype(BF16)
-        for j in range(4):
-            for hf in range(2):
-                pbuf[b, j, hf] = tot[j * quarter:(j + 1) * quarter, cols[hf]:cols[hf] + 512]
-        for slot in (1, 0):
-            for hf in range(2):
-                rs1_copy(b, hf, slot).start()
+                o = (acc[g, half, rs, :] / den).astype(BF16)
+                for j in range(4):
+                    obuf[b, j, half, g] = o[j * quarter:(j + 1) * quarter, :]
+        for hf in range(2):
+            for core in range(2):
+                o_far(b, hf, core).start()
+        for i in range(2):
+            for core in range(2):
+                o_direct(b, i, core).start()
+        o_partner(b).start()
+        orecv[b, y, c] = obuf[b, y, c]
 
     def step1(b):
         for hf in range(2):
-            rs1_copy(b, hf, 1).wait_recv()
-            other = second[hf]
-            sum2[b, hf] = (pbuf[b, other, hf].astype(F32) + rs1[b, hf, 1].astype(F32)).astype(BF16)
-            rs2_copy(b, hf).start()
+            for core in range(2):
+                o_far_wait(b, hf, core)
+            o_relay(b, hf).start()
 
     def step2(b):
         own_rows = pl.ds(pl.multiple_of(b * sub + y * quarter, quarter), quarter)
-        for hf in range(2):
-            rs1_copy(b, hf, 0).wait_recv()
-            rs2_copy(b, hf).wait_recv()
-            tot = pbuf[b, y, hf].astype(F32) + rs1[b, hf, 0].astype(F32) + rs2[b, hf].astype(F32)
-            tot = tot + hid[own_rows, cols[hf]:cols[hf] + 512].astype(F32)
-            xbuf[b, y, hf] = tot.astype(BF16)
+
+        @pl.when(b == 0)
+        def _():
+            for i in range(3):
+                ref = wo.at[(y1, y2, far)[i], pl.ds(pl.multiple_of((1 - c) * w_half, w_half), w_half)]
+                e_copy(ref, ref, 4 + i, {'cp': partner}).wait_recv()
+            for hf in range(2):
+                mlp_rs1(hf, 0).wait_recv()
+                mlp_rs2(hf).wait_recv()
+
+        for i in range(2):
+            for core in range(2):
+                o_direct_wait(b, i, core)
+            o_relay_wait(b, i)
+        o_partner_wait(b)
+        lhs = jnp.concatenate([orecv[b, src, core, g] for src in range(4) for core in range(2) for g in range(2)], axis=1)
+        attn = jnp.dot(lhs, jnp.concatenate([wo[src] for src in range(4)], axis=0), preferred_element_type=F32)
+        for hf in range(2):
+            at = slice(cols[hf], cols[hf] + 512)
+            mlp_tot = mpart[y, hf, b].astype(F32) + mrs1[hf, 0, b].astype(F32) + mrs2[hf, b].astype(F32)
+            out[own_rows, at] = (hid[own_rows, at].astype(F32) + attn[:, at] + mlp_tot).astype(BF16)
             ag1_copy(b, hf).start()
         for hf in range(2):
             ag2_copy(b, hf, 0).start()
 
+    def early_sends():
+        for cpy in caches:
+            cpy.wait()
+        dd_kv(own_ch).wait_send()
+        dd_q(c).wait_send()
+
+        @pl.when(x < 3)
+        def _():
+            kv_copy(own_ch, 0, right).wait_send()
+            kv_copy(own_ch, 1, right).wait_send()
+            kv_copy(oth_ch, 2, right).wait_send()
+
+        @pl.when(x == 0)
+        def _():
+            kv_copy(oth_ch, 3, left).wait_send()
+            kv_copy(oth_ch, 4, left).wait_send()
+
+        @pl.when(x == 1)
+        def _():
+            kv_copy(own_ch, 3, left).wait_send()
+
+        @pl.when(x == 3)
+        def _():
+            kv_copy(own_ch, 0, left).wait_send()
+
+        for i in range(2):
+            wo_direct(i, y).wait_send()
+            wo_relay(i, y1).wait_send()
+            mlp_rs2(i).wait_send()
+            for slot in range(2):
+                mlp_rs1(i, slot).wait_send()
+        for i in range(3):
+            wo_partner(i).wait_send()
+
     def step3(b):
+        o_partner(b).wait_send()
+        for hf in range(2):
+            o_relay(b, hf).wait_send()
+            for slot in range(2):
+                o_direct(b, hf, slot).wait_send()
+                o_far(b, hf, slot).wait_send()
+
+        @pl.when(b == blocks - 1)
+        def _():
+            early_sends()
+
         for hf in range(2):
             ag1_wait(b, hf)
             ag2_copy(b, hf, 1).start()
 
-    def out_copy(b, t, hf):
-        return pltpu.make_async_copy(
-            xbuf.at[b, t, hf],
-            out_hbm.at[pl.ds(b * sub + t * quarter, quarter), pl.ds(cols[hf], 512)],
-            out_sem.at[b, t, hf])
+    def out_copy(b):
+        return pltpu.make_async_copy(out.at[block_rows(b)], out_hbm.at[block_rows(b)], out_sem.at[b])
 
     def step4(b):
+        for hf in range(2):
+            ag1_copy(b, hf).wait_send()
+
+            @pl.when(b > 0)
+            def _():
+                for slot in range(2):
+                    ag2_copy(b - 1, hf, slot).wait_send()
+
         for hf in range(2):
             for slot in range(2):
                 ag2_wait(b, hf, slot)
-        for t in range(4):
-            for hf in range(2):
-                out_copy(b, t, hf).start()
+        out_copy(b).start()
 
     n = 2 * x
 
@@ -400,7 +549,7 @@
         return jnp.where(x == 3, three, near)
 
     three = x == 3
-    lead = 4 * (x // 2) + 2 * (x // 3)
+    lead = 2 * (x // 2) + x // 3
     ticks = lead + 8 + 2 * (x // 3)
 
     def pick(tau, near, far):
@@ -411,33 +560,26 @@
 
     def loop(t, carry):
         tau = t - lead
-        gap = jnp.logical_and(three, jnp.logical_or(tau == 1, tau == 3))
-        s3 = jnp.where(t == 0, 0, jnp.where(t == 1, 1, jnp.where(t == 2, 0, jnp.where(t == 3, 2, jnp.where(
-            t == 4, 3, jnp.where(t == 5, 1, jnp.where(tau == 1, 2, 3)))))))
-        pair3 = jnp.where(jnp.logical_or(t == 2, t >= 5), 1, 0)
-        s = jnp.where(three, s3, t // 2)
-        pair = jnp.where(three, pair3, t % 2)
-
-        @pl.when(jnp.logical_and(x == 2, jnp.logical_and(tau < 0, t % 2 == 0)))
-        def _():
-            kv_copy(chunk_of(s), 0, right).wait_recv()
-
-            @pl.when(t == 2)
-            def _():
-                kv_copy(chunk_of(1), 1, right).start()
-
-        @pl.when(jnp.logical_and(three, jnp.logical_or(t == 0, t == 3)))
+        gap = jnp.logical_and(three, jnp.logical_or(tau == 0, tau == 3))
+        s = jnp.where(t == 2, 2, 0)
+        pair = jnp.where(t == 1, 1, 0)
+
+        @pl.when(jnp.logical_and(tau < 0, t != 1))
         def _():
             ch_b = chunk_of(s + 1)
             kv_copy(ch_b, 0, right).wait_recv()
 
-            @pl.when(t == 0)
+            @pl.when(jnp.logical_and(three, t == 0))
             def _():
                 kv_copy(ch_b, 0, left).start()
 
+            @pl.when(x == 2)
+            def _():
+                kv_copy(ch_b, 1, right).start()
+
             kv_copy(chunk_of(s), 0, right).wait_recv()
 
-        @pl.when(jnp.logical_and(x > 0, tau == 0))
+        @pl.when(jnp.logical_and(x > 0, tau == x // 3))
         def _():
             kv_copy(chunk_of(n - 2), 0, right).wait_recv()
             kv_copy(chunk_of(n - 1), 0, right).wait_recv()
@@ -446,32 +588,52 @@
             def _():
                 kv_copy(chunk_of(1), 3, right).start()
 
-        @pl.when(jnp.logical_or(tau < 0, gap))
+        @pl.when(t == (x // 2) * (x - 1))
+        def _():
+            with jax.named_scope('e2'):
+                for hf in range(2):
+                    mlp_rs1(hf, 1).wait_recv()
+                    msum[hf] = (mpart[second[hf], hf].astype(F32) + mrs1[hf, 1].astype(F32)).astype(BF16)
+                    mlp_rs2(hf).start()
+
+        @pl.when(tau == x // 3)
+        def _():
+            with jax.named_scope('e3'):
+                for hf in range(2):
+                    wo_relay(hf, far).wait_recv()
+                for i in range(3):
+                    wo_partner(i).start()
+
+        @pl.when(tau < 0)
         def _():
             with jax.named_scope('att'):
-                attend_pair(chunk_of(s), pair)
-
-        b0, ok0 = pick(tau, (0, 1, 2, 3), (0, 2, 4, 5))
-
-        @pl.when(jnp.logical_and(ok0, x > 0))
-        def _():
+                attend_pair(chunk_of(s), chunk_of(s + 1), pair)
+
+        b0, ok0 = pick(tau, (0, 1, 2, 3), (1, 2, 4, 5))
+
+        @pl.when(jnp.logical_and(jnp.logical_or(ok0, gap), x > 0))
+        def _():
+            back = jnp.where(gap, 4, 2)
             with jax.named_scope('last'):
-                attend_last(chunk_of(n - 2), chunk_of(n - 1), b0)
-
-        for fn, nm, near, far in ((step1, 's1', (2, 3, 4, 5), (2, 4, 6, 7)),
-                                  (step2, 's2', (3, 4, 5, 6), (3, 5, 7, 8)),
-                                  (step3, 's3', (4, 5, 6, 7), (4, 6, 8, 9))):
-            bk, okk = pick(tau, near, far)
+                attend_last(chunk_of(n - back), chunk_of(n - back + 1), jnp.where(gap, 2 + tau // 3, b0))
+
+        def service(fn, nm, near_t, far_t):
+            bk, okk = pick(tau, near_t, far_t)
 
             @pl.when(okk)
             def _():
                 with jax.named_scope(nm):
                     fn(bk)
 
+        service(step3, 's3', (4, 5, 6, 7), (5, 6, 8, 9))
+        service(step1, 's1', (1, 2, 3, 4), (2, 3, 5, 6))
+
         @pl.when(ok0)
         def _():
             with jax.named_scope('finish'):
                 finish(b0)
+
+        service(step2, 's2', (2, 3, 4, 5), (3, 4, 6, 7))
         return carry
 
     lax.fori_loop(0, ticks, loop, 0)
@@ -483,41 +645,11 @@
 
     lax.fori_loop(0, blocks, last_step, 0)
 
-    dd_kv(own_ch).wait_send()
-    dd_q(c).wait_send()
-    for cpy in caches:
-        cpy.wait()
-
-    @pl.when(x < 3)
-    def _():
-        kv_copy(own_ch, 0, right).wait_send()
-        kv_copy(own_ch, 1, right).wait_send()
-        kv_copy(oth_ch, 2, right).wait_send()
-
-    @pl.when(x == 0)
-    def _():
-        kv_copy(oth_ch, 3, left).wait_send()
-        kv_copy(oth_ch, 4, left).wait_send()
-
-    @pl.when(x == 1)
-    def _():
-        kv_copy(own_ch, 3, left).wait_send()
-
-    @pl.when(x == 3)
-    def _():
-        kv_copy(own_ch, 0, left).wait_send()
-
+    for hf in range(2):
+        for slot in range(2):
+            ag2_copy(blocks - 1, hf, slot).wait_send()
     for b in range(blocks):
-        o_copy(b).wait_send()
-        for hf in range(2):
-            rs2_copy(b, hf).wait_send()
-            ag1_copy(b, hf).wait_send()
-            for slot in range(2):
-                rs1_copy(b, hf, slot).wait_send()
-                ag2_copy(b, hf, slot).wait_send()
-        for t in range(4):
-            for hf in range(2):
-                out_copy(b, t, hf).wait()
+        out_copy(b).wait()
 
 
 def layer(hidden, positions, gain, w_q, w_k, w_v, w_gate, w_up, w_down, w_o):
@@ -537,8 +669,8 @@
         in_specs=[anyspec] * 11,
         out_specs=[anyspec] * 3,
         out_shape=[jax.ShapeDtypeStruct((rows, width), BF16),
-                   jax.ShapeDtypeStruct((rows, w_k.shape[1]), BF16),
-                   jax.ShapeDtypeStruct((rows, w_v.shape[1]), BF16)],
+                   jax.ShapeDtypeStruct((rows * w_k.shape[1] // HEAD_DIM, HEAD_DIM), BF16),
+                   jax.ShapeDtypeStruct((rows * w_v.shape[1] // HEAD_DIM, HEAD_DIM), BF16)],
         scratch_shapes=[
             vm((8, 2, rows, HEAD_DIM), BF16),
             vm((2, 2, rows, HEAD_DIM), BF16),
@@ -556,18 +688,20 @@
             vm((rows, HEAD_DIM), F32),
             vm(w_q.shape, BF16), vm(w_k.shape, BF16), vm(w_v.shape, BF16),
             vm((width, ff), BF16), vm((width, ff), BF16), vm((ff, width), BF16),
-            vm(w_o.shape, BF16),
-            vm((rows, width), F32),
-            vm((rows, w_k.shape[1]), BF16),
-            vm((rows, w_v.shape[1]), BF16),
-            vm((nb, hr, 2 * HEAD_DIM), BF16),
-            vm((nb, hr, 2 * HEAD_DIM), BF16),
-            vm((nb, 4, 2, qr, hw), BF16),
-            vm((nb, 2, 2, qr, hw), BF16),
-            vm((nb, 2, qr, hw), BF16),
-            vm((nb, 2, qr, hw), BF16),
-            vm((nb, 4, 2, qr, hw), BF16),
-            dma((13,)), dma((5,)), dma((8,)), dma((2 + nb,)), dma((2 + nb,)), dma((nb, 12)), dma((nb, 12)), dma((nb, 4, 2)),
+            vm((4,) + w_o.shape, BF16),
+            vm((2, 2 * hr, HEAD_DIM), F32),
+            vm((rows * w_k.shape[1] // HEAD_DIM, HEAD_DIM), BF16),
+            vm((rows * w_v.shape[1] // HEAD_DIM, HEAD_DIM), BF16),
+            vm((4, 2, nb, qr, hw), BF16),
+            vm((2, 2, nb, qr, hw), BF16),
+            vm((2, nb, qr, hw), BF16),
+            vm((2, nb, qr, hw), BF16),
+            vm((nb, 4, 2, 2, qr, HEAD_DIM), BF16),
+            vm((nb, 4, 2, 2, qr, HEAD_DIM), BF16),
+            vm((nb, 2, 2, qr, HEAD_DIM), BF16),
+            vm((rows, width), BF16),
+            dma((13,)), dma((nb,)), dma((5, 2)), dma((8, 2)), dma((2,)), dma((2,)), dma((13,)), dma((13,)),
+            dma((nb, 17)), dma((nb, 17)), dma((nb,)),
         ],
         compiler_params=pltpu.CompilerParams(collective_id=0, has_side_effects=True, vmem_limit_bytes=62 << 20),
         name='layer',

time: 97.6 us -> 90.3 us (0.925)
  Pallas kernels: 91.4 us -> 84.8 us
    pallas_call x1, Pallas kernels: 91.4 us -> 84.8 us  [layer(): pl.pallas_call(layer_kernel, in_specs=[anyspec] * 11, out_specs=[anyspec]...]
    reshape x2 -> x0, local copies, waits for them, and re-layouts: 4.07 us -> none  [the longest x1 2.11 us: local_layer(): kc.reshape(rows, kv_local, HEAD_DIM)]
    unnamed x3 -> x7, local copies, waits for them, and re-layouts: 1.32 us -> 4.76 us
where the time goes in v3:
time: 90.3 us; the launch traced here: 90.2 us
  Pallas kernels  84.8 us (94%)
  local copies, waits for them, and re-layouts  4.76 us (5%)
    pallas_call x1, Pallas kernels, layer(): pl.pallas_call(layer_kernel, in_specs=[anyspec] * 11, out_specs=[anyspec]...  84.8 us
    unnamed x7, local copies, waits for them, and re-layouts  4.76 us

profile of v3, /device:TPU:102, one launch (start us, length us, event | category | flops | bytes accessed | tf_op | source)
XLA Modules:
  0.0 90.2 jit_solution(7781726355478516020)
XLA Ops:
  0.6 84.8 %layer.1 = (bf16[1024,1024]{1,0:T(8,128)(2,1)}, bf16[2048,128]{1,0:T(8,128)(2,1)}, bf16[2048,128]{1,0:T(8,128)(2,1)}) custom-call(bf16[1024,1024]{1,0:T(8,128)(2,1)} %hid_hbm.1, s32[8,128]{1,0:T(8,128)} %bitcast.6, bf16[8,128]{1,0:T(8,128)(2,1)} %bitcast.7, f32[1,128]{1,0:T(1,128)} %constant.2.clone.freq_hbm, bf16[1024,512]{1,0:T(8,128)(2,1)} %wq_hbm.1, ...), custom_call_target="tpu_custom_call" | custom-call | tf_op jit(solution)/shard_map/layer/pallas_call | solution.py:667
  85.4 0.0 copy-start.1
  85.4 0.0 copy-start
  85.4 3.2 %copy.17 = bf16[1024,1024]{1,0:T(8,128)(2,1)} copy(bf16[1024,1024]{1,0:T(8,128)(2,1)} %get-tuple-element.12) | data formatting | bytes 4194304
  88.6 0.0 copy-done.1
  88.6 0.8 copy.18
  89.4 0.0 copy-done
  89.4 0.8 copy.19
Async XLA Ops:
  85.4 3.2 %copy-start.1 = (bf16[2048,128]{1,0:T(8,128)(2,1)S(1)}, bf16[2048,128]{1,0:T(8,128)(2,1)}, u32[]{:S(2)}) copy-start(bf16[2048,128]{1,0:T(8,128)(2,1)} %get-tuple-element.7) | copy-start | bytes 1572868
  85.4 4.0 %copy-start = (bf16[2048,128]{1,0:T(8,128)(2,1)S(1)}, bf16[2048,128]{1,0:T(8,128)(2,1)}, u32[]{:S(2)}) copy-start(bf16[2048,128]{1,0:T(8,128)(2,1)} %get-tuple-element.8) | copy-start | bytes 1572868

commit v4 on v3

--- a/solution.py
+++ b/solution.py
@@ -32,7 +32,7 @@
 
 def layer_kernel(hid_hbm, pos_hbm, gain_hbm, freq_hbm, wq_hbm, wk_hbm, wv_hbm, wg_hbm, wu_hbm, wd_hbm, wo_hbm,
                  out_hbm, kc_hbm, vc_hbm,
-                 kvbuf, qbuf, kvs, qs, acc, mbuf, lbuf, hid, h, pos, gain, freq, cost, sint,
+                 kvbuf, qbuf, acc, mbuf, lbuf, hid, h, pos, gain, freq, cost, sint,
                  wq, wk, wv, wg, wu, wd, wo, wide, kc, vc,
                  mpart, mrs1, msum, mrs2, obuf, orecv, orelay, out,
                  load_sem, hid_sem, kvs_sem, kvr_sem, dds_sem, ddr_sem, es_sem, er_sem, ys_sem, yr_sem, out_sem):
@@ -48,11 +48,12 @@
     rows = hid_hbm.shape[0]
     sub = 256
     blocks = rows // sub
+    straight = 2
     quarter = sub // 4
 
     barrier = pltpu.get_barrier_semaphore()
     for dev in ({'cp': partner}, {'cp': right}, {'cp': left}, {'tp': y1}, {'tp': y2},
-                {'tp': y1, 'cp': partner}, {'tp': y2, 'cp': partner}):
+                {'tp': y1, 'cp': partner}, {'tp': y2, 'cp': partner}, {'tp': 3 - y1}, {'tp': 3 - y1, 'cp': partner}):
         pl.semaphore_signal(barrier, inc=1, device_id=dev, device_id_type=MESH)
 
     pairs = ((hid_hbm, hid), (pos_hbm, pos), (gain_hbm, gain), (freq_hbm, freq), (wk_hbm, wk), (wv_hbm, wv), (wq_hbm, wq),
@@ -77,10 +78,10 @@
                                             device_id=dev, device_id_type=MESH)
 
     def dd_kv(ch):
-        return remote(kvs, kvbuf.at[ch], dds_sem.at[0], ddr_sem.at[0], {'cp': partner})
+        return remote(kvbuf.at[spare], kvbuf.at[ch], dds_sem.at[0], ddr_sem.at[0], {'cp': partner})
 
     def dd_q(half):
-        return remote(qs, qbuf.at[half], dds_sem.at[1], ddr_sem.at[1], {'cp': partner})
+        return remote(qbuf.at[2], qbuf.at[half], dds_sem.at[1], ddr_sem.at[1], {'cp': partner})
 
     class KvCopy:
         def __init__(self, ch, slot, dev):
@@ -137,6 +138,7 @@
         return e_copy(msum.at[hf], mrs2.at[hf], 11 + hf, {'tp': second[hf]})
 
     own_ch = 2 * x + c
+    spare = kvbuf.shape[0] - 1
     oth_ch = 2 * x + 1 - c
 
     loads[1].wait()
@@ -180,19 +182,10 @@
                 wide[slot, pl.ds(g, sub, 2), :] = vals[g].astype(F32)
             out[pair_rows, :] = wide[slot].astype(BF16)
 
-        def place(own, other):
-            kvbuf[own_ch, 0, rs, :] = kk[own]
-            kvbuf[own_ch, 1, rs, :] = vv[own]
-            kvs[0, rs, :] = kk[other]
-            kvs[1, rs, :] = vv[other]
-
-        @pl.when(c == 0)
-        def _():
-            place(0, 1)
-
-        @pl.when(c == 1)
-        def _():
-            place(1, 0)
+        for g in range(2):
+            to = jnp.where(c == g, own_ch, spare)
+            kvbuf[to, 0, rs, :] = kk[g]
+            kvbuf[to, 1, rs, :] = vv[g]
         return carry
 
     def send_own(p):
@@ -207,7 +200,7 @@
     with jax.named_scope('kvproj'):
         lax.fori_loop(0, blocks // 2, project_kv, 0)
     with jax.named_scope('bar'):
-        pl.semaphore_wait(barrier, 7)
+        pl.semaphore_wait(barrier, 9)
     send_own(0)
     with jax.named_scope('kvproj'):
         lax.fori_loop(blocks // 2, blocks, project_kv, 0)
@@ -231,13 +224,7 @@
                 lo = (2 * g + j) * HEAD_DIM
                 qr = rope(q[:, lo:lo + HEAD_DIM], rs)
 
-                @pl.when(c == g)
-                def _():
-                    qbuf[c, j, rs, :] = qr
-
-                @pl.when(c != g)
-                def _():
-                    qs[j, rs, :] = qr
+                qbuf[jnp.where(c == g, c, 2), j, rs, :] = qr
         return carry
 
     with jax.named_scope('qproj'):
@@ -394,6 +381,13 @@
     def o_relay_wait(b, hf):
         y_copy(orelay.at[b, hf], orecv.at[b, far, :, hf], b, 8 + hf, {'tp': y1}).wait_recv()
 
+    def o_beyond(b, core):
+        return remote(obuf.at[b, far, core], orecv.at[b, y, c], ys_sem.at[b, 4 + core], yr_sem.at[b, 4 + c],
+                      {'tp': far, 'cp': 2 * x + core})
+
+    def o_beyond_wait(b, core):
+        y_copy(obuf.at[b, y, c], orecv.at[b, far, core], b, 4 + core, {'tp': far}).wait_recv()
+
     def o_partner(b):
         return y_copy(obuf.at[b, y, 1 - c], orecv.at[b, y, c], b, 10, {'cp': partner})
 
@@ -427,9 +421,17 @@
                 o = (acc[g, half, rs, :] / den).astype(BF16)
                 for j in range(4):
                     obuf[b, j, half, g] = o[j * quarter:(j + 1) * quarter, :]
-        for hf in range(2):
+        @pl.when(b < straight)
+        def _():
+            for hf in range(2):
+                for core in range(2):
+                    o_far(b, hf, core).start()
+
+        @pl.when(b >= straight)
+        def _():
             for core in range(2):
-                o_far(b, hf, core).start()
+                o_beyond(b, core).start()
+
         for i in range(2):
             for core in range(2):
                 o_direct(b, i, core).start()
@@ -437,10 +439,12 @@
         orecv[b, y, c] = obuf[b, y, c]
 
     def step1(b):
-        for hf in range(2):
-            for core in range(2):
-                o_far_wait(b, hf, core)
-            o_relay(b, hf).start()
+        @pl.when(b < straight)
+        def _():
+            for hf in range(2):
+                for core in range(2):
+                    o_far_wait(b, hf, core)
+                o_relay(b, hf).start()
 
     def step2(b):
         own_rows = pl.ds(pl.multiple_of(b * sub + y * quarter, quarter), quarter)
@@ -457,7 +461,17 @@
         for i in range(2):
             for core in range(2):
                 o_direct_wait(b, i, core)
-            o_relay_wait(b, i)
+
+        @pl.when(b < straight)
+        def _():
+            for hf in range(2):
+                o_relay_wait(b, hf)
+
+        @pl.when(b >= straight)
+        def _():
+            for core in range(2):
+                o_beyond_wait(b, core)
+
         o_partner_wait(b)
         lhs = jnp.concatenate([orecv[b, src, core, g] for src in range(4) for core in range(2) for g in range(2)], axis=1)
         attn = jnp.dot(lhs, jnp.concatenate([wo[src] for src in range(4)], axis=0), preferred_element_type=F32)
@@ -505,11 +519,21 @@
 
     def step3(b):
         o_partner(b).wait_send()
-        for hf in range(2):
-            o_relay(b, hf).wait_send()
-            for slot in range(2):
-                o_direct(b, hf, slot).wait_send()
-                o_far(b, hf, slot).wait_send()
+        for i in range(2):
+            for core in range(2):
+                o_direct(b, i, core).wait_send()
+
+        @pl.when(b < straight)
+        def _():
+            for hf in range(2):
+                o_relay(b, hf).wait_send()
+                for core in range(2):
+                    o_far(b, hf, core).wait_send()
+
+        @pl.when(b >= straight)
+        def _():
+            for core in range(2):
+                o_beyond(b, core).wait_send()
 
         @pl.when(b == blocks - 1)
         def _():
@@ -633,7 +657,7 @@
             with jax.named_scope('finish'):
                 finish(b0)
 
-        service(step2, 's2', (2, 3, 4, 5), (3, 4, 6, 7))
+        service(step2, 's2', (2, 3, 4, 5), (3, 4, 5, 7))
         return carry
 
     lax.fori_loop(0, ticks, loop, 0)
@@ -645,11 +669,13 @@
 
     lax.fori_loop(0, blocks, last_step, 0)
 
-    for hf in range(2):
-        for slot in range(2):
-            ag2_copy(blocks - 1, hf, slot).wait_send()
-    for b in range(blocks):
-        out_copy(b).wait()
+    with jax.named_scope('sends'):
+        for hf in range(2):
+            for slot in range(2):
+                ag2_copy(blocks - 1, hf, slot).wait_send()
+    with jax.named_scope('outs'):
+        for b in range(blocks):
+            out_copy(b).wait()
 
 
 def layer(hidden, positions, gain, w_q, w_k, w_v, w_gate, w_up, w_down, w_o):
@@ -672,10 +698,8 @@
                    jax.ShapeDtypeStruct((rows * w_k.shape[1] // HEAD_DIM, HEAD_DIM), BF16),
                    jax.ShapeDtypeStruct((rows * w_v.shape[1] // HEAD_DIM, HEAD_DIM), BF16)],
         scratch_shapes=[
-            vm((8, 2, rows, HEAD_DIM), BF16),
-            vm((2, 2, rows, HEAD_DIM), BF16),
-            vm((2, rows, HEAD_DIM), BF16),
-            vm((2, rows, HEAD_DIM), BF16),
+            vm((9, 2, rows, HEAD_DIM), BF16),
+            vm((3, 2, rows, HEAD_DIM), BF16),
             vm((2, 2, rows, HEAD_DIM), F32),
             vm((2, 2, rows, HEAD_DIM), F32),
             vm((2, 2, rows, HEAD_DIM), F32),

time: 90.3 us -> 88.4 us (0.979)
  Pallas kernels: 84.8 us -> 82.9 us
    pallas_call x1, Pallas kernels: 84.8 us -> 82.9 us  [layer(): pl.pallas_call(layer_kernel, in_specs=[anyspec] * 11, out_specs=[anyspec]...]
where the time goes in v4:
time: 88.4 us; the launch traced here: 88.3 us
  Pallas kernels  82.9 us (94%)
  local copies, waits for them, and re-layouts  4.76 us (5%)
    pallas_call x1, Pallas kernels, layer(): pl.pallas_call(layer_kernel, in_specs=[anyspec] * 11, out_specs=[anyspec]...  82.9 us
    unnamed x7, local copies, waits for them, and re-layouts  4.76 us

profile of v4, /device:TPU:102, one launch (start us, length us, event | category | flops | bytes accessed | tf_op | source)
XLA Modules:
  0.0 88.3 jit_solution(17728577768141635594)
XLA Ops:
  0.6 82.9 %layer.1 = (bf16[1024,1024]{1,0:T(8,128)(2,1)}, bf16[2048,128]{1,0:T(8,128)(2,1)}, bf16[2048,128]{1,0:T(8,128)(2,1)}) custom-call(bf16[1024,1024]{1,0:T(8,128)(2,1)} %hid_hbm.1, s32[8,128]{1,0:T(8,128)} %bitcast.6, bf16[8,128]{1,0:T(8,128)(2,1)} %bitcast.7, f32[1,128]{1,0:T(1,128)} %constant.2.clone.freq_hbm, bf16[1024,512]{1,0:T(8,128)(2,1)} %wq_hbm.1, ...), custom_call_target="tpu_custom_call" | custom-call | tf_op jit(solution)/shard_map/layer/pallas_call | solution.py:693
  83.5 0.0 copy-start.1
  83.5 0.0 copy-start
  83.6 3.2 %copy.17 = bf16[1024,1024]{1,0:T(8,128)(2,1)} copy(bf16[1024,1024]{1,0:T(8,128)(2,1)} %get-tuple-element.12) | data formatting | bytes 4194304
  86.7 0.0 copy-done.1
  86.7 0.8 copy.18
  87.5 0.0 copy-done
  87.5 0.8 copy.19
Async XLA Ops:
  83.5 3.2 %copy-start.1 = (bf16[2048,128]{1,0:T(8,128)(2,1)S(1)}, bf16[2048,128]{1,0:T(8,128)(2,1)}, u32[]{:S(2)}) copy-start(bf16[2048,128]{1,0:T(8,128)(2,1)} %get-tuple-element.7) | copy-start | bytes 1572868
  83.5 4.0 %copy-start = (bf16[2048,128]{1,0:T(8,128)(2,1)S(1)}, bf16[2048,128]{1,0:T(8,128)(2,1)}, u32[]{:S(2)}) copy-start(bf16[2048,128]{1,0:T(8,128)(2,1)} %get-tuple-element.8) | copy-start | bytes 1572868

commit v5 on v4

--- a/solution.py
+++ b/solution.py
@@ -81,26 +81,25 @@
         return remote(kvbuf.at[spare], kvbuf.at[ch], dds_sem.at[0], ddr_sem.at[0], {'cp': partner})
 
     def dd_q(half):
-        return remote(qbuf.at[2], qbuf.at[half], dds_sem.at[1], ddr_sem.at[1], {'cp': partner})
+        return remote(qbuf.at[2], qbuf.at[half], dds_sem.at[0], ddr_sem.at[1], {'cp': partner})
+
+    def bytes_of(ref, ss, rsem):
+        return remote(ref, ref, ss, rsem, {'cp': partner})
 
     class KvCopy:
         def __init__(self, ch, slot, dev):
             self.parts = []
             for p in range(2):
                 ref = kvbuf.at[ch, :, pl.ds(p * (rows // 2), rows // 2)]
-                self.parts.append(remote(ref, ref, kvs_sem.at[slot, p], kvr_sem.at[ch, p], {'cp': dev}))
+                self.parts.append(remote(ref, ref, kvs_sem.at[0], kvr_sem.at[ch], {'cp': dev}))
+            self.whole = bytes_of(kvbuf.at[ch], kvs_sem.at[0], kvr_sem.at[ch])
 
         def start(self):
             for part in self.parts:
                 part.start()
 
         def wait_recv(self):
-            for part in self.parts:
-                part.wait_recv()
-
-        def wait_send(self):
-            for part in self.parts:
-                part.wait_send()
+            self.whole.wait_recv()
 
     kv_copy = KvCopy
 
@@ -109,7 +108,7 @@
     far = 3 - y1
 
     def e_copy(src, dst, i, dev):
-        return remote(src, dst, es_sem.at[i], er_sem.at[i], dev)
+        return remote(src, dst, es_sem.at[0], er_sem.at[i], dev)
 
     w_half = 2 * HEAD_DIM
 
@@ -122,20 +121,20 @@
 
     def wo_relay(hf, shard):
         ref = wo_rows(shard, hf * HEAD_DIM, HEAD_DIM)
-        return e_copy(ref, ref, 2 + hf, {'tp': first[hf]})
+        return e_copy(ref, ref, 2, {'tp': first[hf]})
 
     def wo_partner(i):
         ref = wo_rows((y1, y2, far)[i], 0, w_half)
-        return e_copy(ref, ref, 4 + i, {'cp': partner})
+        return e_copy(ref, ref, 3, {'cp': partner})
 
     def mlp_rs1(hf, slot):
         dev = first[hf]
         beyond = (3 - dev) if hf == 0 else (dev + 1 - 2 * (dev % 2))
         tile = dev if slot == 0 else beyond
-        return e_copy(mpart.at[tile, hf], mrs1.at[hf, slot], 7 + 2 * hf + slot, {'tp': dev})
+        return e_copy(mpart.at[tile, hf], mrs1.at[hf, slot], 4 + (hf if slot else 2), {'tp': dev})
 
     def mlp_rs2(hf):
-        return e_copy(msum.at[hf], mrs2.at[hf], 11 + hf, {'tp': second[hf]})
+        return e_copy(msum.at[hf], mrs2.at[hf], 7, {'tp': second[hf]})
 
     own_ch = 2 * x + c
     spare = kvbuf.shape[0] - 1
@@ -359,59 +358,39 @@
         attend((ch_a, ch_b), [(g, half, block_rows(b)) for half in range(2) for g in range(2)])
 
     def y_copy(src, dst, b, i, dev):
-        return remote(src, dst, ys_sem.at[b, i], yr_sem.at[b, i], dev)
+        return remote(src, dst, ys_sem.at[b], yr_sem.at[b, i], dev)
 
     def o_direct(b, i, core):
-        return remote(obuf.at[b, first[i], core], orecv.at[b, y, c], ys_sem.at[b, 2 * i + core], yr_sem.at[b, 2 * i + c],
+        return remote(obuf.at[b, first[i], core], orecv.at[b, y, c], ys_sem.at[b], yr_sem.at[b, 0],
                       {'tp': first[i], 'cp': 2 * x + core})
 
-    def o_direct_wait(b, i, core):
-        y_copy(obuf.at[b, y, c], orecv.at[b, first[i], core], b, 2 * i + core, {'tp': y1}).wait_recv()
-
     def o_far(b, hf, core):
-        return remote(obuf.at[b, far, core, hf], orelay.at[b, hf, c], ys_sem.at[b, 4 + 2 * hf + core], yr_sem.at[b, 4 + 2 * hf + c],
+        return remote(obuf.at[b, far, core, hf], orelay.at[b, hf, c], ys_sem.at[b], yr_sem.at[b, 1],
                       {'tp': first[hf], 'cp': 2 * x + core})
 
-    def o_far_wait(b, hf, core):
-        y_copy(obuf.at[b, far, core, hf], orelay.at[b, hf, core], b, 4 + 2 * hf + core, {'tp': y1}).wait_recv()
-
     def o_relay(b, hf):
-        return y_copy(orelay.at[b, hf], orecv.at[b, first[hf], :, hf], b, 8 + hf, {'tp': second[hf]})
-
-    def o_relay_wait(b, hf):
-        y_copy(orelay.at[b, hf], orecv.at[b, far, :, hf], b, 8 + hf, {'tp': y1}).wait_recv()
+        return y_copy(orelay.at[b, hf], orecv.at[b, first[hf], :, hf], b, 0, {'tp': second[hf]})
 
     def o_beyond(b, core):
-        return remote(obuf.at[b, far, core], orecv.at[b, y, c], ys_sem.at[b, 4 + core], yr_sem.at[b, 4 + c],
+        return remote(obuf.at[b, far, core], orecv.at[b, y, c], ys_sem.at[b], yr_sem.at[b, 0],
                       {'tp': far, 'cp': 2 * x + core})
 
-    def o_beyond_wait(b, core):
-        y_copy(obuf.at[b, y, c], orecv.at[b, far, core], b, 4 + core, {'tp': far}).wait_recv()
-
     def o_partner(b):
-        return y_copy(obuf.at[b, y, 1 - c], orecv.at[b, y, c], b, 10, {'cp': partner})
-
-    def o_partner_wait(b):
-        y_copy(obuf.at[b, y, c], orecv.at[b, y, 1 - c], b, 10, {'cp': partner}).wait_recv()
+        return y_copy(obuf.at[b, y, 1 - c], orecv.at[b, y, c], b, 0, {'cp': partner})
 
     def xt(b, t, hf):
         return out.at[pl.ds(pl.multiple_of(b * sub + t * quarter, quarter), quarter), pl.ds(cols[hf], 512)]
 
     def ag1_copy(b, hf):
-        return y_copy(xt(b, y, hf), xt(b, y, hf), b, 11 + hf, {'tp': second[hf]})
+        return y_copy(xt(b, y, hf), xt(b, y, hf), b, 2 + hf, {'tp': second[hf]})
 
     def ag1_wait(b, hf):
         t = second[hf]
-        y_copy(xt(b, t, hf), xt(b, t, hf), b, 11 + hf, {'tp': t}).wait_recv()
+        y_copy(xt(b, t, hf), xt(b, t, hf), b, 2 + hf, {'tp': t}).wait_recv()
 
     def ag2_copy(b, hf, slot):
         t = y if slot == 0 else second[hf]
-        return y_copy(xt(b, t, hf), xt(b, t, hf), b, 13 + 2 * hf + slot, {'tp': first[hf]})
-
-    def ag2_wait(b, hf, slot):
-        dev = first[hf]
-        t = dev if slot == 0 else far
-        y_copy(xt(b, t, hf), xt(b, t, hf), b, 13 + 2 * hf + slot, {'tp': dev}).wait_recv()
+        return y_copy(xt(b, t, hf), xt(b, t, hf), b, 4, {'tp': first[hf]})
 
     def finish(b):
         rs = block_rows(b)
@@ -441,9 +420,8 @@
     def step1(b):
         @pl.when(b < straight)
         def _():
+            bytes_of(orelay.at[b], ys_sem.at[b], yr_sem.at[b, 1]).wait_recv()
             for hf in range(2):
-                for core in range(2):
-                    o_far_wait(b, hf, core)
                 o_relay(b, hf).start()
 
     def step2(b):
@@ -451,28 +429,11 @@
 
         @pl.when(b == 0)
         def _():
-            for i in range(3):
-                ref = wo.at[(y1, y2, far)[i], pl.ds(pl.multiple_of((1 - c) * w_half, w_half), w_half)]
-                e_copy(ref, ref, 4 + i, {'cp': partner}).wait_recv()
-            for hf in range(2):
-                mlp_rs1(hf, 0).wait_recv()
-                mlp_rs2(hf).wait_recv()
-
-        for i in range(2):
-            for core in range(2):
-                o_direct_wait(b, i, core)
-
-        @pl.when(b < straight)
-        def _():
-            for hf in range(2):
-                o_relay_wait(b, hf)
-
-        @pl.when(b >= straight)
-        def _():
-            for core in range(2):
-                o_beyond_wait(b, core)
-
-        o_partner_wait(b)
+            bytes_of(wo.at[pl.ds(0, 3), pl.ds(0, w_half)], es_sem.at[0], er_sem.at[3]).wait_recv()
+            bytes_of(mrs1.at[:, 0], es_sem.at[0], er_sem.at[6]).wait_recv()
+            bytes_of(mrs2, es_sem.at[0], er_sem.at[7]).wait_recv()
+
+        bytes_of(hid.at[pl.ds(0, 7 * quarter // 4)], ys_sem.at[b], yr_sem.at[b, 0]).wait_recv()
         lhs = jnp.concatenate([orecv[b, src, core, g] for src in range(4) for core in range(2) for g in range(2)], axis=1)
         attn = jnp.dot(lhs, jnp.concatenate([wo[src] for src in range(4)], axis=0), preferred_element_type=F32)
         for hf in range(2):
@@ -486,55 +447,15 @@
     def early_sends():
         for cpy in caches:
             cpy.wait()
-        dd_kv(own_ch).wait_send()
-        dd_q(c).wait_send()
-
-        @pl.when(x < 3)
-        def _():
-            kv_copy(own_ch, 0, right).wait_send()
-            kv_copy(own_ch, 1, right).wait_send()
-            kv_copy(oth_ch, 2, right).wait_send()
-
-        @pl.when(x == 0)
-        def _():
-            kv_copy(oth_ch, 3, left).wait_send()
-            kv_copy(oth_ch, 4, left).wait_send()
-
-        @pl.when(x == 1)
-        def _():
-            kv_copy(own_ch, 3, left).wait_send()
-
-        @pl.when(x == 3)
-        def _():
-            kv_copy(own_ch, 0, left).wait_send()
-
-        for i in range(2):
-            wo_direct(i, y).wait_send()
-            wo_relay(i, y1).wait_send()
-            mlp_rs2(i).wait_send()
-            for slot in range(2):
-                mlp_rs1(i, slot).wait_send()
-        for i in range(3):
-            wo_partner(i).wait_send()
+        for i in range(4):
+            @pl.when(x == i)
+            def _():
+                bytes_of(kvbuf.at[pl.ds(0, (5, 4, 3, 1)[i])], kvs_sem.at[0], kvr_sem.at[0]).wait_send()
+
+        bytes_of(kvbuf.at[pl.ds(0, 2)], dds_sem.at[0], ddr_sem.at[0]).wait_send()
+        bytes_of(kvbuf.at[pl.ds(0, 9)], es_sem.at[0], er_sem.at[0]).wait_send()
 
     def step3(b):
-        o_partner(b).wait_send()
-        for i in range(2):
-            for core in range(2):
-                o_direct(b, i, core).wait_send()
-
-        @pl.when(b < straight)
-        def _():
-            for hf in range(2):
-                o_relay(b, hf).wait_send()
-                for core in range(2):
-                    o_far(b, hf, core).wait_send()
-
-        @pl.when(b >= straight)
-        def _():
-            for core in range(2):
-                o_beyond(b, core).wait_send()
-
         @pl.when(b == blocks - 1)
         def _():
             early_sends()
@@ -544,20 +465,10 @@
             ag2_copy(b, hf, 1).start()
 
     def out_copy(b):
-        return pltpu.make_async_copy(out.at[block_rows(b)], out_hbm.at[block_rows(b)], out_sem.at[b])
+        return pltpu.make_async_copy(out.at[block_rows(b)], out_hbm.at[block_rows(b)], out_sem.at[0])
 
     def step4(b):
-        for hf in range(2):
-            ag1_copy(b, hf).wait_send()
-
-            @pl.when(b > 0)
-            def _():
-                for slot in range(2):
-                    ag2_copy(b - 1, hf, slot).wait_send()
-
-        for hf in range(2):
-            for slot in range(2):
-                ag2_wait(b, hf, slot)
+        bytes_of(hid.at[pl.ds(0, 2 * quarter)], ys_sem.at[b], yr_sem.at[b, 4]).wait_recv()
         out_copy(b).start()
 
     n = 2 * x
@@ -623,8 +534,7 @@
         @pl.when(tau == x // 3)
         def _():
             with jax.named_scope('e3'):
-                for hf in range(2):
-                    wo_relay(hf, far).wait_recv()
+                bytes_of(wo.at[far, pl.ds(0, w_half)], es_sem.at[0], er_sem.at[2]).wait_recv()
                 for i in range(3):
                     wo_partner(i).start()
 
@@ -669,13 +579,10 @@
 
     lax.fori_loop(0, blocks, last_step, 0)
 
-    with jax.named_scope('sends'):
-        for hf in range(2):
-            for slot in range(2):
-                ag2_copy(blocks - 1, hf, slot).wait_send()
-    with jax.named_scope('outs'):
-        for b in range(blocks):
-            out_copy(b).wait()
+    for b in range(blocks):
+        pieces = 7 + 12 + (2 if b < straight else 0)
+        bytes_of(hid.at[pl.ds(0, pieces * quarter // 4)], ys_sem.at[b], yr_sem.at[b, 0]).wait_send()
+    pltpu.make_async_copy(out, out_hbm, out_sem.at[0]).wait()
 
 
 def layer(hidden, positions, gain, w_q, w_k, w_v, w_gate, w_up, w_down, w_o):
@@ -724,8 +631,8 @@
             vm((nb, 4, 2, 2, qr, HEAD_DIM), BF16),
             vm((nb, 2, 2, qr, HEAD_DIM), BF16),
             vm((rows, width), BF16),
-            dma((13,)), dma((nb,)), dma((5, 2)), dma((8, 2)), dma((2,)), dma((2,)), dma((13,)), dma((13,)),
-            dma((nb, 17)), dma((nb, 17)), dma((nb,)),
+            dma((13,)), dma((nb,)), dma((1,)), dma((8,)), dma((1,)), dma((2,)), dma((1,)), dma((8,)),
+            dma((nb,)), dma((nb, 5)), dma((1,)),
         ],
         compiler_params=pltpu.CompilerParams(collective_id=0, has_side_effects=True, vmem_limit_bytes=62 << 20),
         name='layer',

time: 88.4 us -> 87.2 us (0.986)
  Pallas kernels: 82.9 us -> 81.7 us
    pallas_call x1, Pallas kernels: 82.9 us -> 81.7 us  [layer(): pl.pallas_call(layer_kernel, in_specs=[anyspec] * 11, out_specs=[anyspec]...]
where the time goes in v5:
time: 87.2 us; the launch traced here: 87.1 us
  Pallas kernels  81.7 us (94%)
  local copies, waits for them, and re-layouts  4.76 us (5%)
    pallas_call x1, Pallas kernels, layer(): pl.pallas_call(layer_kernel, in_specs=[anyspec] * 11, out_specs=[anyspec]...  81.7 us
    unnamed x7, local copies, waits for them, and re-layouts  4.76 us

profile of v5, /device:TPU:102, one launch (start us, length us, event | category | flops | bytes accessed | tf_op | source)
XLA Modules:
  0.0 87.1 jit_solution(16567932028743713363)
XLA Ops:
  0.6 81.7 %layer.1 = (bf16[1024,1024]{1,0:T(8,128)(2,1)}, bf16[2048,128]{1,0:T(8,128)(2,1)}, bf16[2048,128]{1,0:T(8,128)(2,1)}) custom-call(bf16[1024,1024]{1,0:T(8,128)(2,1)} %hid_hbm.1, s32[8,128]{1,0:T(8,128)} %bitcast.6, bf16[8,128]{1,0:T(8,128)(2,1)} %bitcast.7, f32[1,128]{1,0:T(1,128)} %constant.2.clone.freq_hbm, bf16[1024,512]{1,0:T(8,128)(2,1)} %wq_hbm.1, ...), custom_call_target="tpu_custom_call" | custom-call | tf_op jit(solution)/shard_map/layer/pallas_call | solution.py:600
  82.3 0.0 copy-start.1
  82.3 0.0 copy-start
  82.3 3.2 %copy.17 = bf16[1024,1024]{1,0:T(8,128)(2,1)} copy(bf16[1024,1024]{1,0:T(8,128)(2,1)} %get-tuple-element.12) | data formatting | bytes 4194304
  85.5 0.0 copy-done.1
  85.5 0.8 copy.18
  86.3 0.0 copy-done
  86.3 0.8 copy.19
Async XLA Ops:
  82.3 3.2 %copy-start.1 = (bf16[2048,128]{1,0:T(8,128)(2,1)S(1)}, bf16[2048,128]{1,0:T(8,128)(2,1)}, u32[]{:S(2)}) copy-start(bf16[2048,128]{1,0:T(8,128)(2,1)} %get-tuple-element.7) | copy-start | bytes 1572868
  82.3 4.0 %copy-start = (bf16[2048,128]{1,0:T(8,128)(2,1)S(1)}, bf16[2048,128]{1,0:T(8,128)(2,1)}, u32[]{:S(2)}) copy-start(bf16[2048,128]{1,0:T(8,128)(2,1)} %get-tuple-element.8) | copy-start | bytes 1572868

commit v6 on v5

--- a/solution.py
+++ b/solution.py
@@ -154,12 +154,12 @@
     for i in (2, 4, 5):
         loads[i].wait()
 
-    even = lax.broadcasted_iota(jnp.int32, (sub, HEAD_DIM), 1) % 2 == 0
     gain_f = gain[...].astype(F32)
     gain_row = jnp.concatenate([gain_f[i:i + 1, :] for i in range(gain.shape[0])], axis=1)
 
     def rope(col, rs):
         u = col.astype(BF16).astype(F32)
+        even = lax.broadcasted_iota(jnp.int32, u.shape, 1) % 2 == 0
         swapped = jnp.where(even, pltpu.roll(u, HEAD_DIM - 1, 1), pltpu.roll(u, 1, 1))
         return (u * cost[rs, :] + swapped * sint[rs, :]).astype(BF16)
 
@@ -216,7 +216,7 @@
     loads[6].wait()
 
     def project_q(i, carry):
-        rs = pl.ds(pl.multiple_of(i * sub, sub), sub)
+        rs = pl.ds(pl.multiple_of(i * 2 * sub, 2 * sub), 2 * sub)
         q = jnp.dot(h[rs, :], wq[...], preferred_element_type=F32)
         for g in range(2):
             for j in range(2):
@@ -227,7 +227,7 @@
         return carry
 
     with jax.named_scope('qproj'):
-        lax.fori_loop(0, rows // sub, project_q, 0)
+        lax.fori_loop(0, rows // (2 * sub), project_q, 0)
     dd_q(c).start()
     dd_kv(oth_ch).wait_recv()
 
@@ -246,19 +246,21 @@
     cols = (0, 512)
 
     def mlp(i, carry):
-        rs = pl.ds(pl.multiple_of(i * sub, sub), sub)
+        rs = pl.ds(pl.multiple_of(i * 2 * sub, 2 * sub), 2 * sub)
         hh = h[rs, :]
         gate = jnp.dot(hh, wg[...], preferred_element_type=F32).astype(BF16).astype(F32)
         up = jnp.dot(hh, wu[...], preferred_element_type=F32).astype(BF16).astype(F32)
         a = (gate * (1.0 / (1.0 + jnp.exp(-gate))) * up).astype(BF16)
         tot = jnp.dot(a, wd[...], preferred_element_type=F32).astype(BF16)
-        for j in range(4):
-            for hf in range(2):
-                mpart[j, hf, i] = tot[j * quarter:(j + 1) * quarter, cols[hf]:cols[hf] + 512]
+        for k in range(2):
+            for j in range(4):
+                lo = k * sub + j * quarter
+                for hf in range(2):
+                    mpart[j, hf, 2 * i + k] = tot[lo:lo + quarter, cols[hf]:cols[hf] + 512]
         return carry
 
     with jax.named_scope('mlp'):
-        lax.fori_loop(0, rows // sub, mlp, 0)
+        lax.fori_loop(0, rows // (2 * sub), mlp, 0)
 
     for slot in (1, 0):
         for hf in range(2):

time: 87.2 us -> 86.7 us (level)
  no operation moved by 1% of the time
where the time goes in v6:
time: 86.7 us; the launch traced here: 86.6 us
  Pallas kernels  81.2 us (94%)
  local copies, waits for them, and re-layouts  4.76 us (5%)
    pallas_call x1, Pallas kernels, layer(): pl.pallas_call(layer_kernel, in_specs=[anyspec] * 11, out_specs=[anyspec]...  81.2 us
    unnamed x7, local copies, waits for them, and re-layouts  4.76 us

profile of v6, /device:TPU:102, one launch (start us, length us, event | category | flops | bytes accessed | tf_op | source)
XLA Modules:
  0.0 86.6 jit_solution(9968786344430517933)
XLA Ops:
  0.6 81.2 %layer.1 = (bf16[1024,1024]{1,0:T(8,128)(2,1)}, bf16[2048,128]{1,0:T(8,128)(2,1)}, bf16[2048,128]{1,0:T(8,128)(2,1)}) custom-call(bf16[1024,1024]{1,0:T(8,128)(2,1)} %hid_hbm.1, s32[8,128]{1,0:T(8,128)} %bitcast.6, bf16[8,128]{1,0:T(8,128)(2,1)} %bitcast.7, f32[1,128]{1,0:T(1,128)} %constant.2.clone.freq_hbm, bf16[1024,512]{1,0:T(8,128)(2,1)} %wq_hbm.1, ...), custom_call_target="tpu_custom_call" | custom-call | tf_op jit(solution)/shard_map/layer/pallas_call | solution.py:602
  81.8 0.0 copy-start.1
  81.8 0.0 copy-start
  81.8 3.2 %copy.17 = bf16[1024,1024]{1,0:T(8,128)(2,1)} copy(bf16[1024,1024]{1,0:T(8,128)(2,1)} %get-tuple-element.12) | data formatting | bytes 4194304
  85.0 0.0 copy-done.1
  85.0 0.8 copy.18
  85.8 0.0 copy-done
  85.8 0.8 copy.19
Async XLA Ops:
  81.8 3.2 %copy-start.1 = (bf16[2048,128]{1,0:T(8,128)(2,1)S(1)}, bf16[2048,128]{1,0:T(8,128)(2,1)}, u32[]{:S(2)}) copy-start(bf16[2048,128]{1,0:T(8,128)(2,1)} %get-tuple-element.7) | copy-start | bytes 1572868
  81.8 4.0 %copy-start = (bf16[2048,128]{1,0:T(8,128)(2,1)S(1)}, bf16[2048,128]{1,0:T(8,128)(2,1)}, u32[]{:S(2)}) copy-start(bf16[2048,128]{1,0:T(8,128)(2,1)} %get-tuple-element.8) | copy-start | bytes 1572868
